TPU v7x, 32 devices: a whole 2x2x4 slice. The times are simulated.
32 devices in a mesh: pod: 2 (over x), dp: 4 (over z), sp: 4 (over y, core).
Axes of the slice: x: 2, y: 2, z: 4, core: 2. Of those that a mesh axis runs over, the one named last changes fastest.
Arguments:
- images: bfloat16 [128, 32, 168, 128], P(('pod', 'dp'), 'sp'), parts along dimension 0
- w_a: bfloat16 [1, 3, 3, 128, 128], replicated
- norm_a: float32 [1, 2, 128], replicated
- w_down: bfloat16 [3, 3, 128, 256], replicated
- norm_down: float32 [2, 256], replicated
- w_b: bfloat16 [3, 3, 3, 256, 256], replicated
- norm_b: float32 [3, 2, 256], replicated
Outputs:
- output: bfloat16 [128, 16, 84, 256], P(('pod', 'dp'), 'sp'), parts along dimension 0
There are 2 independent parts. A program takes and returns all parts, laid end to end along the dimension named above; an argument that names none is the same for every part.
All inputs are finite; a program needn't handle non-finite values.
Results may differ from a plain program's by a relative error of at most 0.00736.
Values are sent between devices in bfloat16 or wider.
A program may use at most 1 GiB of HBM per device.

v0:
```python
import jax
import jax.numpy as jnp
from jax import lax
from jax.sharding import PartitionSpec as P

EPS_VALUE = 1e-5
CONV_DIMS = ('NHWC', 'HWIO', 'NHWC')


def solution(mesh):
    group_size = mesh.shape['sp']
    data_size = mesh.shape['dp']
    to_lower = [(dev_idx, dev_idx + 1) for dev_idx in range(group_size - 1)]
    to_upper = [(dev_idx + 1, dev_idx) for dev_idx in range(group_size - 1)]

    def batch_norm(z_val, norm_pair):
        local_sums = jnp.stack([jnp.sum(z_val, axis=(0, 1, 2)), jnp.sum(z_val * z_val, axis=(0, 1, 2))])
        group_sums = lax.psum(local_sums, ('dp', 'sp'))
        elem_count = z_val.shape[0] * z_val.shape[1] * z_val.shape[2] * data_size * group_size
        mean_val = group_sums[0] / elem_count
        var_val = group_sums[1] / elem_count - mean_val * mean_val
        scaled = norm_pair[0] * (z_val - mean_val) * lax.rsqrt(var_val + EPS_VALUE) + norm_pair[1]
        return jnp.maximum(scaled, 0.0).astype(jnp.bfloat16)

    def same_layer(hidden, weight, norm_pair):
        top_rows = lax.ppermute(hidden[:, -1:], 'sp', to_lower)
        bottom_rows = lax.ppermute(hidden[:, :1], 'sp', to_upper)
        padded = jnp.concatenate([top_rows, hidden, bottom_rows], axis=1)
        z_val = lax.conv_general_dilated(padded, weight, (1, 1), ((0, 0), (1, 1)), dimension_numbers=CONV_DIMS, preferred_element_type=jnp.float32)
        return batch_norm(z_val, norm_pair)

    def down_layer(hidden, weight, norm_pair):
        bottom_rows = lax.ppermute(hidden[:, :1], 'sp', to_upper)
        padded = jnp.concatenate([hidden, bottom_rows], axis=1)
        z_val = lax.conv_general_dilated(padded, weight, (2, 2), ((0, 0), (0, 1)), dimension_numbers=CONV_DIMS, preferred_element_type=jnp.float32)
        return batch_norm(z_val, norm_pair)

    def local_stack(row_tile, w_a, norm_a, w_down, norm_down, w_b, norm_b):
        hidden = row_tile
        for layer_idx in range(w_a.shape[0]):
            hidden = same_layer(hidden, w_a[layer_idx], norm_a[layer_idx])
        hidden = down_layer(hidden, w_down, norm_down)
        for layer_idx in range(w_b.shape[0]):
            hidden = same_layer(hidden, w_b[layer_idx], norm_b[layer_idx])
        return hidden

    act_spec = P(('pod', 'dp'), 'sp', None, None)
    return jax.shard_map(local_stack, mesh=mesh, in_specs=(act_spec, P(), P(), P(), P(), P(), P()), out_specs=act_spec, check_vma=False)
```

profile of v0, /device:TPU:0, one launch (start us, length us, event | category | flops | bytes accessed | tf_op | source)
XLA Modules:
  0.0 293.0 jit_solution(23954809037570807)
XLA Ops:
  0.0 6.2 %copy.8 = bf16[16,8,168,128]{3,0,2,1:T(8,128)(2,1)S(1)} copy(bf16[16,8,168,128]{3,2,1,0:T(8,128)(2,1)} %param.7) | data formatting | bytes 11010048 | tf_op args[0]
  6.4 2.5 collective-permute-start
  10.6 4.4 %collective-permute-done.1 = bf16[16,1,168,128]{3,0,2,1:T(8,128)(2,1)S(1)} collective-permute-done((bf16[16,1,168,128]{3,0,2,1:T(8,128)(2,1)S(1)}, bf16[16,1,168,128]{3,0,2,1:T(8,128)(2,1)S(1)}, u32[]{:S(2)}, u32[]{:S(2)}) %collective-permute-start.1) | collective-permute-done | bytes 688160 | tf_op jit(solution)/shard_map/ppermute | solution.py:27
  15.0 15.8 %fusion.42 = (f32[128]{0:T(128)S(1)}, f32[128]{0:T(128)S(1)}, f32[16,8,168,128]{3,0,2,1:T(8,128)}) fusion(bf16[1,3,3,128,128]{4,3,2,1,0:T(8,128)(2,1)S(1)} %copy-done.5, bf16[16,1,168,128]{3,0,2,1:T(8,128)(2,1)S(1)} %collective-permute-done.1, bf16[16,8,168,128]{3,0,2,1:T(8,128)(2,1)S(1)} %copy.8, bf16[16,1,168,128]{3,0,2,1:T(8,128)(2,1)S(1)} %collective-permute-done), kind=kOutput, calls=%fused_computation.73 | convolution fusion | flops 6345523200 | bytes 18187264 | tf_op jit(solution)/shard_map/conv_general_dilated | solution.py:29
  30.8 38.4 %psum.35 = f32[2,128]{1,0:T(2,128)S(1)} all-reduce(f32[2,128]{1,0:T(2,128)S(1)} %pad_maximum_fusion.4), channel_id=1, replica_groups=mesh['pod'=2,'dp'=4,'sp'=4] {'dp','sp'}, use_global_device_ids=true, to_apply=%region_2.0 | all-reduce | flops 256 | bytes 2048 | tf_op jit(solution)/shard_map/psum | solution.py:18
  69.2 6.4 %maximum_convert_fusion = bf16[16,8,168,128]{3,0,2,1:T(8,128)(2,1)S(1)} fusion(f32[16,8,168,128]{3,0,2,1:T(8,128)} %get-tuple-element.41, f32[128]{0:T(128)S(1)} %get-tuple-element.40, f32[128]{0:T(128)S(1)} %fusion.36, f32[128]{0:T(128)S(1)} %multiply_bitcast_fusion, f32[128]{0:T(128)S(1)} %get-tuple-element.39), kind=kLoop, calls=%fused_computation | loop fusion | flops 16515072 | bytes 16517120 | tf_op jit(solution)/shard_map/convert_element_type | solution.py:23
  77.1 2.7 collective-permute-done.2
  79.9 5.5 %fusion.46 = (f32[256]{0:T(256)S(1)}, f32[256]{0:T(256)S(1)}, f32[16,4,84,256]{3,0,2,1:T(8,128)}) fusion(bf16[3,3,128,256]{3,2,1,0:T(8,128)(2,1)S(1)} %copy-done, bf16[16,1,168,128]{3,0,2,1:T(8,128)(2,1)S(1)} %collective-permute-done.2, bf16[16,8,168,128]{3,0,2,1:T(8,128)(2,1)S(1)} %maximum_convert_fusion), kind=kOutput, calls=%fused_computation.77 | convolution fusion | flops 3174825472 | bytes 12290048 | tf_op jit(solution)/shard_map/conv_general_dilated | solution.py:35
  85.4 36.0 %psum.36 = f32[2,256]{1,0:T(2,128)S(1)} all-reduce(f32[2,256]{1,0:T(2,128)S(1)} %pad_maximum_fusion), channel_id=1, replica_groups=mesh['pod'=2,'dp'=4,'sp'=4] {'dp','sp'}, use_global_device_ids=true, to_apply=%region_5.0 | all-reduce | flops 512 | bytes 4096 | tf_op jit(solution)/shard_map/psum | solution.py:18
  121.4 3.6 %maximum_convert_fusion.4 = bf16[16,4,84,256]{3,0,2,1:T(8,128)(2,1)S(1)} fusion(f32[16,4,84,256]{3,0,2,1:T(8,128)} %get-tuple-element.42, f32[256]{0:T(256)S(1)} %bitcast.76, f32[256]{0:T(256)S(1)} %add_rsqrt_fusion.3, f32[256]{0:T(256)S(1)} %bitcast.62, f32[256]{0:T(256)S(1)} %bitcast.75), kind=kLoop, calls=%fused_computation.18 | loop fusion | flops 8257536 | bytes 8261632 | tf_op jit(solution)/shard_map/convert_element_type | solution.py:23
  128.1 2.3 collective-permute-done.4
  130.5 10.2 %fusion.45 = (f32[256]{0:T(256)S(1)}, f32[256]{0:T(256)S(1)}, f32[16,4,84,256]{3,0,2,1:T(8,128)}) fusion(bf16[3,3,3,256,256]{4,3,2,1,0:T(8,128)(2,1)} %param.12, bf16[16,1,84,256]{3,0,2,1:T(8,128)(2,1)S(1)} %collective-permute-done.4, bf16[16,4,84,256]{3,0,2,1:T(8,128)(2,1)S(1)} %maximum_convert_fusion.4, ...), kind=kOutput, calls=%fused_computation.76 | convolution fusion | flops 6307971072 | bytes 10815488 | tf_op jit(solution)/shard_map/conv_general_dilated | solution.py:29
  140.7 35.5 %psum.37 = f32[2,256]{1,0:T(2,128)S(1)} all-reduce(f32[2,256]{1,0:T(2,128)S(1)} %pad_maximum_fusion.1), channel_id=1, replica_groups=mesh['pod'=2,'dp'=4,'sp'=4] {'dp','sp'}, use_global_device_ids=true, to_apply=%region_8.0 | all-reduce | flops 512 | bytes 4096 | tf_op jit(solution)/shard_map/psum | solution.py:18
  176.2 3.6 %maximum_convert_fusion.3 = bf16[16,4,84,256]{3,0,2,1:T(8,128)(2,1)S(1)} fusion(f32[16,4,84,256]{3,0,2,1:T(8,128)} %get-tuple-element.43, f32[256]{0:T(256)S(1)} %bitcast.73, f32[256]{0:T(256)S(1)} %add_rsqrt_fusion.2, f32[256]{0:T(256)S(1)} %bitcast.66, f32[256]{0:T(256)S(1)} %bitcast.74), kind=kLoop, calls=%fused_computation.16 | loop fusion | flops 8257536 | bytes 8261632 | tf_op jit(solution)/shard_map/convert_element_type | solution.py:23
  181.2 1.5 collective-permute-start.6
  182.9 2.3 collective-permute-done.6
  185.2 10.2 %fusion.44 = (f32[256]{0:T(256)S(1)}, f32[256]{0:T(256)S(1)}, f32[16,4,84,256]{3,0,2,1:T(8,128)}) fusion(bf16[3,3,3,256,256]{4,3,2,1,0:T(8,128)(2,1)} %param.12, bf16[16,1,84,256]{3,0,2,1:T(8,128)(2,1)S(1)} %collective-permute-done.6, bf16[16,4,84,256]{3,0,2,1:T(8,128)(2,1)S(1)} %maximum_convert_fusion.3, ...), kind=kOutput, calls=%fused_computation.75 | convolution fusion | flops 6307971072 | bytes 10815488 | tf_op jit(solution)/shard_map/conv_general_dilated | solution.py:29
  195.5 35.5 %psum.38 = f32[2,256]{1,0:T(2,128)S(1)} all-reduce(f32[2,256]{1,0:T(2,128)S(1)} %pad_maximum_fusion.2), channel_id=1, replica_groups=mesh['pod'=2,'dp'=4,'sp'=4] {'dp','sp'}, use_global_device_ids=true, to_apply=%region_11.0 | all-reduce | flops 512 | bytes 4096 | tf_op jit(solution)/shard_map/psum | solution.py:18
  231.0 3.6 %maximum_convert_fusion.2 = bf16[16,4,84,256]{3,0,2,1:T(8,128)(2,1)S(1)} fusion(f32[16,4,84,256]{3,0,2,1:T(8,128)} %get-tuple-element.44, f32[256]{0:T(256)S(1)} %bitcast.72, f32[256]{0:T(256)S(1)} %add_rsqrt_fusion.1, f32[256]{0:T(256)S(1)} %bitcast.68, f32[256]{0:T(256)S(1)} %bitcast.71), kind=kLoop, calls=%fused_computation.14 | loop fusion | flops 8257536 | bytes 8261632 | tf_op jit(solution)/shard_map/convert_element_type | solution.py:23
  237.7 2.3 collective-permute-done.8
  240.0 10.2 %fusion.43 = (f32[256]{0:T(256)S(1)}, f32[256]{0:T(256)S(1)}, f32[16,4,84,256]{3,0,2,1:T(8,128)}) fusion(bf16[3,3,3,256,256]{4,3,2,1,0:T(8,128)(2,1)} %param.12, bf16[16,1,84,256]{3,0,2,1:T(8,128)(2,1)S(1)} %collective-permute-done.8, bf16[16,4,84,256]{3,0,2,1:T(8,128)(2,1)S(1)} %maximum_convert_fusion.2, ...), kind=kOutput, calls=%fused_computation.74 | convolution fusion | flops 6307971072 | bytes 10815488 | tf_op jit(solution)/shard_map/conv_general_dilated | solution.py:29
  250.3 35.5 %psum.39 = f32[2,256]{1,0:T(2,128)S(1)} all-reduce(f32[2,256]{1,0:T(2,128)S(1)} %pad_maximum_fusion.3), channel_id=1, replica_groups=mesh['pod'=2,'dp'=4,'sp'=4] {'dp','sp'}, use_global_device_ids=true, to_apply=%region_14.0 | all-reduce | flops 512 | bytes 4096 | tf_op jit(solution)/shard_map/psum | solution.py:18
  285.7 3.6 %maximum_convert_fusion.1 = bf16[16,4,84,256]{3,0,2,1:T(8,128)(2,1)S(1)} fusion(f32[16,4,84,256]{3,0,2,1:T(8,128)} %get-tuple-element.45, f32[256]{0:T(256)S(1)} %bitcast.70, f32[256]{0:T(256)S(1)} %add_rsqrt_fusion, f32[256]{0:T(256)S(1)} %bitcast.64, f32[256]{0:T(256)S(1)} %bitcast.69), kind=kLoop, calls=%fused_computation.12 | loop fusion | flops 8257536 | bytes 8261632 | tf_op jit(solution)/shard_map/convert_element_type | solution.py:23
  289.4 3.7 %copy.11 = bf16[16,4,84,256]{3,1,2,0:T(4,128)(2,1)} copy(bf16[16,4,84,256]{3,0,2,1:T(8,128)(2,1)S(1)} %maximum_convert_fusion.1) | data formatting | bytes 5505024 | tf_op jit(solution)/shard_map/convert_element_type | solution.py:23
  (46 shorter events, 11.3 us)
Async XLA Ops:
  0.0 79.9 %copy-start = (bf16[3,3,128,256]{3,2,1,0:T(8,128)(2,1)S(1)}, bf16[3,3,128,256]{3,2,1,0:T(8,128)(2,1)}, u32[]{:S(2)}) copy-start(bf16[3,3,128,256]{3,2,1,0:T(8,128)(2,1)} %param.10) | copy-start | bytes 1769476
  0.0 10.2 %copy-start.4 = (f32[1,2,128]{2,1,0:T(2,128)S(1)}, f32[1,2,128]{2,1,0:T(2,128)}, u32[]{:S(2)}) copy-start(f32[1,2,128]{2,1,0:T(2,128)} %param.9) | copy-start | bytes 3076
  0.0 15.0 %copy-start.5 = (bf16[1,3,3,128,128]{4,3,2,1,0:T(8,128)(2,1)S(1)}, bf16[1,3,3,128,128]{4,3,2,1,0:T(8,128)(2,1)}, u32[]{:S(2)}) copy-start(bf16[1,3,3,128,128]{4,3,2,1,0:T(8,128)(2,1)} %param.8) | copy-start | bytes 884740
  6.4 4.2 %collective-permute-start = (bf16[16,1,168,128]{3,0,2,1:T(8,128)(2,1)S(1)}, bf16[16,1,168,128]{3,0,2,1:T(8,128)(2,1)S(1)}, u32[]{:S(2)}, u32[]{:S(2)}) collective-permute-start(bf16[16,1,168,128]{3,0,2,1:T(8,128)(2,1)S(1)} %get-tuple-element.15), channel_id=1, source_target_pairs={{0,1},{1,2},{2,3},{4,5},{5,6},{6,7},{8,9},{9,10},{10,11},{12,13},{... | collective-permute-start | bytes 2064392 | tf_op jit(solution)/shard_map/ppermute | solution.py:26
  8.9 6.1 %collective-permute-start.1 = (bf16[16,1,168,128]{3,0,2,1:T(8,128)(2,1)S(1)}, bf16[16,1,168,128]{3,0,2,1:T(8,128)(2,1)S(1)}, u32[]{:S(2)}, u32[]{:S(2)}) collective-permute-start(bf16[16,1,168,128]{3,0,2,1:T(8,128)(2,1)S(1)} %get-tuple-element.16), channel_id=1, source_target_pairs={{1,0},{2,1},{3,2},{5,4},{6,5},{7,6},{9,8},{10,9},{11,10},{13,12},{... | collective-permute-start | bytes 2064392 | tf_op jit(solution)/shard_map/ppermute | solution.py:27
  69.2 7.9 %copy-start.3 = (f32[2,256]{1,0:T(2,128)S(1)}, f32[2,256]{1,0:T(2,128)}, u32[]{:S(2)}) copy-start(f32[2,256]{1,0:T(2,128)} %param.11) | copy-start | bytes 6148
  75.8 4.0 %collective-permute-start.2 = (bf16[16,1,168,128]{3,0,2,1:T(8,128)(2,1)S(1)}, bf16[16,1,168,128]{3,0,2,1:T(8,128)(2,1)S(1)}, u32[]{:S(2)}, u32[]{:S(2)}) collective-permute-start(bf16[16,1,168,128]{3,0,2,1:T(8,128)(2,1)S(1)} %slice.147), channel_id=1, source_target_pairs={{1,0},{2,1},{3,2},{5,4},{6,5},{7,6},{9,8},{10,9},{11,10},{13,12},{... | collective-permute-start | bytes 2064392 | tf_op jit(solution)/shard_map/ppermute | solution.py:33
  121.4 6.3 %copy-start.2 = (f32[3,2,256]{2,1,0:T(2,128)S(1)}, f32[3,2,256]{2,1,0:T(2,128)}, u32[]{:S(2)}) copy-start(f32[3,2,256]{2,1,0:T(2,128)} %param.13) | copy-start | bytes 18436
  125.1 3.1 %collective-permute-start.3 = (bf16[16,1,84,256]{3,0,2,1:T(8,128)(2,1)S(1)}, bf16[16,1,84,256]{3,0,2,1:T(8,128)(2,1)S(1)}, u32[]{:S(2)}, u32[]{:S(2)}) collective-permute-start(bf16[16,1,84,256]{3,0,2,1:T(8,128)(2,1)S(1)} %get-tuple-element.21), channel_id=1, source_target_pairs={{0,1},{1,2},{2,3},{4,5},{5,6},{6,7},{8,9},{9,10},{10,11},{12,13},{... | collective-permute-start | bytes 2064392 | tf_op jit(solution)/shard_map/ppermute | solution.py:26
  126.4 4.0 %collective-permute-start.4 = (bf16[16,1,84,256]{3,0,2,1:T(8,128)(2,1)S(1)}, bf16[16,1,84,256]{3,0,2,1:T(8,128)(2,1)S(1)}, u32[]{:S(2)}, u32[]{:S(2)}) collective-permute-start(bf16[16,1,84,256]{3,0,2,1:T(8,128)(2,1)S(1)} %get-tuple-element.22), channel_id=1, source_target_pairs={{1,0},{2,1},{3,2},{5,4},{6,5},{7,6},{9,8},{10,9},{11,10},{13,12},{... | collective-permute-start | bytes 2064392 | tf_op jit(solution)/shard_map/ppermute | solution.py:27
  179.9 3.1 %collective-permute-start.5 = (bf16[16,1,84,256]{3,0,2,1:T(8,128)(2,1)S(1)}, bf16[16,1,84,256]{3,0,2,1:T(8,128)(2,1)S(1)}, u32[]{:S(2)}, u32[]{:S(2)}) collective-permute-start(bf16[16,1,84,256]{3,0,2,1:T(8,128)(2,1)S(1)} %get-tuple-element.19), channel_id=1, source_target_pairs={{0,1},{1,2},{2,3},{4,5},{5,6},{6,7},{8,9},{9,10},{10,11},{12,13},{... | collective-permute-start | bytes 2064392 | tf_op jit(solution)/shard_map/ppermute | solution.py:26
  181.2 4.0 %collective-permute-start.6 = (bf16[16,1,84,256]{3,0,2,1:T(8,128)(2,1)S(1)}, bf16[16,1,84,256]{3,0,2,1:T(8,128)(2,1)S(1)}, u32[]{:S(2)}, u32[]{:S(2)}) collective-permute-start(bf16[16,1,84,256]{3,0,2,1:T(8,128)(2,1)S(1)} %get-tuple-element.20), channel_id=1, source_target_pairs={{1,0},{2,1},{3,2},{5,4},{6,5},{7,6},{9,8},{10,9},{11,10},{13,12},{... | collective-permute-start | bytes 2064392 | tf_op jit(solution)/shard_map/ppermute | solution.py:27
  234.6 3.1 %collective-permute-start.7 = (bf16[16,1,84,256]{3,0,2,1:T(8,128)(2,1)S(1)}, bf16[16,1,84,256]{3,0,2,1:T(8,128)(2,1)S(1)}, u32[]{:S(2)}, u32[]{:S(2)}) collective-permute-start(bf16[16,1,84,256]{3,0,2,1:T(8,128)(2,1)S(1)} %get-tuple-element.17), channel_id=1, source_target_pairs={{0,1},{1,2},{2,3},{4,5},{5,6},{6,7},{8,9},{9,10},{10,11},{12,13},{... | collective-permute-start | bytes 2064392 | tf_op jit(solution)/shard_map/ppermute | solution.py:26
  236.0 4.0 %collective-permute-start.8 = (bf16[16,1,84,256]{3,0,2,1:T(8,128)(2,1)S(1)}, bf16[16,1,84,256]{3,0,2,1:T(8,128)(2,1)S(1)}, u32[]{:S(2)}, u32[]{:S(2)}) collective-permute-start(bf16[16,1,84,256]{3,0,2,1:T(8,128)(2,1)S(1)} %get-tuple-element.18), channel_id=1, source_target_pairs={{1,0},{2,1},{3,2},{5,4},{6,5},{7,6},{9,8},{10,9},{11,10},{13,12},{... | collective-permute-start | bytes 2064392 | tf_op jit(solution)/shard_map/ppermute | solution.py:27
  285.7 7.3 %copy-start.1 = (bf16[3,3,128,256]{3,2,1,0:T(8,128)(2,1)S(1)}, bf16[3,3,128,256]{3,2,1,0:T(8,128)(2,1)}, u32[]{:S(2)}) copy-start(bf16[3,3,128,256]{3,2,1,0:T(8,128)(2,1)} %param.10) | copy-start | bytes 1769476
where the time goes:
time: 294 us; the launch traced here: 293 us
  blocking collectives  181 us (62%)
  matrix products  52 us (18%)
  other arithmetic  21 us (7%)
  waiting for transfers between devices  15.5 us (5%)
  starting transfers between devices  13.1 us (4%)
  local copies, waits for them, and re-layouts  10.5 us (4%)
    psum x5, blocking collectives, batch_norm(): group_sums = lax.psum(local_sums, ('dp', 'sp'))  181 us
    conv_general_dilated x4, matrix products, same_layer(): lax.conv_general_dilated(padded, weight, (1, 1), ((0, 0), (1, 1)), dimens...  46.4 us
    convert_element_type x5, other arithmetic, batch_norm(): return jnp.maximum(scaled, 0.0).astype(jnp.bfloat16)  20.8 us
    ppermute x4, waiting for transfers between devices, same_layer(): bottom_rows = lax.ppermute(hidden[:, :1], 'sp', to_upper)  11.4 us
    ppermute x4, starting transfers between devices, same_layer(): top_rows = lax.ppermute(hidden[:, -1:], 'sp', to_lower)  6.47 us
    unnamed x13, local copies, waits for them, and re-layouts  6.21 us
  transfers between devices with their start and end apart: 9, of which 9 were waited for; matrix products, arithmetic and copies ran while one was open for 0% of the time, Pallas kernels for 0%

commit v1 on v0

v1 whole, which is shorter than its diff:
```python
import functools

import jax
import jax.numpy as jnp
from jax import lax
from jax.experimental import pallas as pl
from jax.experimental.pallas import tpu as pltpu
from jax.sharding import PartitionSpec as P

EPS_VALUE = 1e-5
MESH = pl.DeviceIdType.MESH
BF16 = jnp.bfloat16
F32 = jnp.float32


def stack_kernel(n_dp, n_sp, img, wa, na, wd, nd, wb, nb, out,
                 nat, stage, img_t, act_a, act_b, zbuf, zfin, out_nat,
                 wa_v, wd_v, wb_v, stat_src, stat_dst,
                 in_sem, w_sem, halo_in_send, halo_in_recv, stat_send, stat_recv,
                 halo_send, halo_recv, out_sem):
    n_img, n_row, width, ch_a = img.shape
    n_out_row, w_out, ch_b = out.shape[1], out.shape[2], out.shape[3]
    n_layers_b = wb.shape[0]
    n_group = n_dp * n_sp
    m_row = w_out * n_img
    my_pod, my_dp, my_sp = lax.axis_index("pod"), lax.axis_index("dp"), lax.axis_index("sp")
    me = my_dp * n_sp + my_sp
    is_top = my_sp == 0
    is_bottom = my_sp == n_sp - 1
    not_top = my_sp > 0
    not_bottom = my_sp < n_sp - 1
    upper = (my_pod, my_dp, lax.max(my_sp - 1, 0))
    lower = (my_pod, my_dp, lax.min(my_sp + 1, n_sp - 1))

    def peer(offset):
        flat = lax.rem(me + offset, n_group)
        return (my_pod, flat // n_sp, lax.rem(flat, n_sp))

    row_copies = [pltpu.make_async_copy(img.at[:, r], nat.at[r + 1], in_sem.at[r]) for r in range(n_row)]
    for c in row_copies:
        c.start()
    w_copies = []
    for p in range(3):
        for q in range(3):
            for half in range(2):
                k = q + half
                w_copies.append(pltpu.make_async_copy(
                    wa.at[p, q], wa_v.at[pl.ds(p * 4 * ch_a + k * ch_a, ch_a), pl.ds(half * ch_a, ch_a)],
                    w_sem.at[len(w_copies)]))
    for p in range(3):
        for q in range(3):
            off = p * 2 * ch_a + q * ch_a if q < 2 else 6 * ch_a + p * ch_a
            w_copies.append(pltpu.make_async_copy(wd.at[p, q], wd_v.at[pl.ds(off, ch_a)], w_sem.at[len(w_copies)]))
    w_copies.append(pltpu.make_async_copy(wb, wb_v, w_sem.at[len(w_copies)]))
    for c in w_copies:
        c.start()

    barrier = pltpu.get_barrier_semaphore()
    for i in range(1, n_group):
        pl.semaphore_signal(barrier, inc=1, device_id=peer(i), device_id_type=MESH)

    for p in range(3):
        wa_v[pl.ds(p * 4 * ch_a + 3 * ch_a, ch_a), 0:ch_a] = jnp.zeros((ch_a, ch_a), BF16)
        wa_v[pl.ds(p * 4 * ch_a, ch_a), ch_a:2 * ch_a] = jnp.zeros((ch_a, ch_a), BF16)
    n_rows_t = img_t.shape[0]
    img_t[:, 0, :, 0:ch_a] = jnp.zeros((n_rows_t, n_img, ch_a), BF16)
    img_t[:, w_out, :, ch_a:2 * ch_a] = jnp.zeros((n_rows_t, n_img, ch_a), BF16)
    act_a[:, w_out] = jnp.zeros((act_a.shape[0], n_img, 2 * ch_a), BF16)
    act_b[:, 0] = jnp.zeros((act_b.shape[0], n_img, ch_b), BF16)
    act_b[:, w_out + 1] = jnp.zeros((act_b.shape[0], n_img, ch_b), BF16)

    @pl.when(is_top)
    def _():
        nat[0] = jnp.zeros((n_img, width, ch_a), BF16)
        act_b[0] = jnp.zeros((w_out + 2, n_img, ch_b), BF16)

    @pl.when(is_bottom)
    def _():
        nat[n_row + 1] = jnp.zeros((n_img, width, ch_a), BF16)
        nat[n_row + 2] = jnp.zeros((n_img, width, ch_a), BF16)
        act_b[n_out_row + 1] = jnp.zeros((w_out + 2, n_img, ch_b), BF16)

    pl.semaphore_wait(barrier, n_group - 1)

    def image_halo(src_row, dst_row, dev, k):
        return pltpu.make_async_remote_copy(
            src_ref=img.at[:, src_row], dst_ref=nat.at[dst_row], send_sem=halo_in_send.at[k],
            recv_sem=halo_in_recv.at[k], device_id=dev, device_id_type=MESH)

    to_lower = image_halo(n_row - 1, 0, lower, 0)
    to_upper0 = image_halo(0, n_row + 1, upper, 1)
    to_upper1 = image_halo(1, n_row + 2, upper, 2)

    @pl.when(not_bottom)
    def _():
        to_lower.start()

    @pl.when(not_top)
    def _():
        to_upper0.start()
        to_upper1.start()

    def transpose_row(k):
        pitch = stage.shape[0] // n_img

        for i in range(n_img):
            stage[pl.ds(i * pitch, width), :] = nat[k, i].astype(F32)
        for x in range(width):
            half = (x + 1) % 2
            img_t[k, (x + 1) // 2, :, half * ch_a:(half + 1) * ch_a] = (
                stage[pl.ds(x, n_img, stride=pitch), :].astype(BF16))

    def fold(total, z_val):
        z3 = z_val.reshape(m_row // 8, 8, ch_b)
        return total[0] + jnp.sum(z3, axis=0), total[1] + jnp.sum(z3 * z3, axis=0)

    def conv_a(r):
        parts = []
        for p in range(3):
            for k in range(2):
                parts.append(img_t[r + p, pl.ds(k, w_out)].reshape(m_row, 2 * ch_a))
        return jnp.dot(jnp.concatenate(parts, axis=1), wa_v[...], preferred_element_type=F32)

    def conv_down(r):
        parts = [act_a[2 * r + p, pl.ds(0, w_out)].reshape(m_row, 2 * ch_a) for p in range(3)]
        parts += [act_a[2 * r + p, pl.ds(1, w_out), :, 0:ch_a].reshape(m_row, ch_a) for p in range(3)]
        return jnp.dot(jnp.concatenate(parts, axis=1), wd_v[...], preferred_element_type=F32)

    def conv_b(r, layer):
        parts = []
        for p in range(3):
            for q in range(3):
                parts.append(act_b[r + p, pl.ds(q, w_out)].reshape(m_row, ch_b))
        return jnp.dot(jnp.concatenate(parts, axis=1), wb_v[layer], preferred_element_type=F32)

    def run_rows(rows, conv, total, keep):
        first, step, count = rows

        def body(i, total):
            r = first + i * step
            z_val = conv(r)
            keep(r, z_val)
            return fold(total, z_val)

        return lax.fori_loop(0, count, body, total)

    def keep_z(r, z_val):
        zbuf[r] = z_val

    def keep_final(r, z_val):
        pitch = zfin.shape[1] // (n_out_row * w_out)
        for x in range(w_out):
            for h in range(ch_b // 128):
                zfin[h, pl.ds((r * w_out + x) * pitch, n_img), :] = z_val[x * n_img:(x + 1) * n_img, h * 128:(h + 1) * 128]

    def send_stats(layer, total):
        s1 = jnp.sum(total[0], axis=0, keepdims=True)
        s2 = jnp.sum(total[1], axis=0, keepdims=True)
        if layer == 0:
            s1 = s1[:, :ch_a] + s1[:, ch_a:]
            s2 = s2[:, :ch_a] + s2[:, ch_a:]
            s1 = jnp.concatenate([s1, s1], axis=1)
            s2 = jnp.concatenate([s2, s2], axis=1)
        both = jnp.concatenate([s1, s2], axis=0)
        stat_src[layer] = both
        stat_dst[layer, me] = both
        copies = []
        for i in range(1, n_group):
            copies.append(pltpu.make_async_remote_copy(
                src_ref=stat_src.at[layer], dst_ref=stat_dst.at[layer, me], send_sem=stat_send.at[layer, i],
                recv_sem=stat_recv.at[layer, i], device_id=peer(i), device_id_type=MESH))
        for c in copies:
            c.start()
        return copies

    def finish_stats(layer, copies, gamma, beta, count):
        for c in copies:
            c.wait()
        tot = jnp.sum(stat_dst[layer], axis=0)
        mean = tot[0:1] / count
        var = tot[1:2] / count - mean * mean
        scale = gamma * lax.rsqrt(var + EPS_VALUE)
        return mean, scale, beta

    def normalize(z_val, coef):
        mean, scale, beta = coef
        return jnp.maximum((z_val - mean) * scale + beta, 0.0).astype(BF16)

    zeros = (jnp.zeros((8, ch_b), F32), jnp.zeros((8, ch_b), F32))

    for c in row_copies:
        c.wait()

    def t_body(k, carry):
        transpose_row(k)
        return carry

    lax.fori_loop(1, n_row + 1, t_body, 0)
    for c in w_copies:
        c.wait()
    total = run_rows((1, 1, n_row - 2), conv_a, zeros, keep_z)

    @pl.when(not_top)
    def _():
        to_lower.wait_recv()

    @pl.when(not_bottom)
    def _():
        to_upper0.wait_recv()
        to_upper1.wait_recv()

    def t_body_halo(k, carry):
        transpose_row(jnp.where(k == 0, 0, n_row + k))
        return carry

    lax.fori_loop(0, 3, t_body_halo, 0)
    total = run_rows((0, n_row - 1, 2), conv_a, total, keep_z)
    copies = send_stats(0, total)
    zbuf[n_row] = conv_a(n_row)
    n_a = float(n_group * n_img * n_row * width)
    wide = lambda v: jnp.concatenate([v, v], axis=1)
    coef = finish_stats(0, copies, wide(na[0, 0:1]), wide(na[0, 1:2]), n_a)

    def norm_a_body(r, carry):
        act_a[r, pl.ds(0, w_out)] = normalize(zbuf[r], coef).reshape(w_out, n_img, 2 * ch_a)
        return carry

    lax.fori_loop(0, n_row + 1, norm_a_body, 0)

    @pl.when(is_bottom)
    def _():
        act_a[n_row] = jnp.zeros((w_out + 1, n_img, 2 * ch_a), BF16)

    total = run_rows((0, 1, n_out_row), conv_down, zeros, keep_z)
    copies = send_stats(1, total)
    n_b = float(n_group * m_row * n_out_row)
    coef = finish_stats(1, copies, nd[0:1], nd[1:2], n_b)

    for layer in range(n_layers_b):
        def norm_b_row(r):
            act_b[r + 1, pl.ds(1, w_out)] = normalize(zbuf[r], coef).reshape(w_out, n_img, ch_b)

        down = pltpu.make_async_remote_copy(
            src_ref=act_b.at[n_out_row, pl.ds(1, w_out)], dst_ref=act_b.at[0, pl.ds(1, w_out)],
            send_sem=halo_send.at[layer, 0], recv_sem=halo_recv.at[layer, 0], device_id=lower, device_id_type=MESH)
        up = pltpu.make_async_remote_copy(
            src_ref=act_b.at[1, pl.ds(1, w_out)], dst_ref=act_b.at[n_out_row + 1, pl.ds(1, w_out)],
            send_sem=halo_send.at[layer, 1], recv_sem=halo_recv.at[layer, 1], device_id=upper, device_id_type=MESH)

        norm_b_row(0)

        @pl.when(not_top)
        def _():
            up.start()

        norm_b_row(n_out_row - 1)

        @pl.when(not_bottom)
        def _():
            down.start()

        def norm_b_body(r, carry):
            norm_b_row(r)
            return carry

        lax.fori_loop(1, n_out_row - 1, norm_b_body, 0)
        last = layer == n_layers_b - 1
        conv = functools.partial(conv_b, layer=layer)
        keep = keep_final if last else keep_z
        total = run_rows((1, 1, n_out_row - 2), conv, zeros, keep)

        @pl.when(not_top)
        def _():
            up.wait_send()
            down.wait_recv()

        @pl.when(not_bottom)
        def _():
            down.wait_send()
            up.wait_recv()

        total = run_rows((0, n_out_row - 1, 2), conv, total, keep)
        copies = send_stats(2 + layer, total)
        coef = finish_stats(2 + layer, copies, nb[layer, 0:1], nb[layer, 1:2], n_b)

    pitch = zfin.shape[1] // (n_out_row * w_out)

    def out_body(r, carry):
        for i in range(n_img):
            for h in range(ch_b // 128):
                lanes = slice(h * 128, (h + 1) * 128)
                z_val = zfin[h, pl.ds(r * w_out * pitch + i, w_out, stride=pitch), :]
                out_nat[r, i, :, lanes] = normalize(z_val, tuple(v[:, lanes] for v in coef))
        pltpu.make_async_copy(out_nat.at[r], out.at[:, r], out_sem.at[r]).start()
        return carry

    lax.fori_loop(0, n_out_row, out_body, 0)
    for r in range(n_out_row):
        pltpu.make_async_copy(out_nat.at[r], out.at[:, r], out_sem.at[r]).wait()

    @pl.when(not_bottom)
    def _():
        to_lower.wait_send()

    @pl.when(not_top)
    def _():
        to_upper0.wait_send()
        to_upper1.wait_send()


def solution(mesh):
    n_sp, n_dp = mesh.shape['sp'], mesh.shape['dp']

    def local_stack(img, w_a, norm_a, w_down, norm_down, w_b, norm_b):
        n_img, n_row, width, ch_a = img.shape
        ch_b = w_down.shape[-1]
        n_out_row, w_out = n_row // 2, width // 2
        n_layers_b = w_b.shape[0]
        n_group = n_sp * n_dp
        any_spec = pl.BlockSpec(memory_space=pl.ANY)
        vmem_spec = pl.BlockSpec(memory_space=pltpu.VMEM)
        dma = pltpu.SemaphoreType.DMA
        n_stats = 2 + n_layers_b
        return pl.pallas_call(
            functools.partial(stack_kernel, n_dp, n_sp),
            out_shape=jax.ShapeDtypeStruct((n_img, n_out_row, w_out, ch_b), BF16),
            in_specs=[any_spec, any_spec, vmem_spec, any_spec, vmem_spec, any_spec, vmem_spec],
            out_specs=any_spec,
            scratch_shapes=[
                pltpu.VMEM((n_row + 3, n_img, width, ch_a), BF16),
                pltpu.VMEM((n_img * width, 128), F32),
                pltpu.VMEM((n_row + 3, w_out + 1, n_img, 2 * ch_a), BF16),
                pltpu.VMEM((n_row + 1, w_out + 1, n_img, 2 * ch_a), BF16),
                pltpu.VMEM((n_out_row + 2, w_out + 2, n_img, ch_b), BF16),
                pltpu.VMEM((n_row + 1, w_out * n_img, ch_b), F32),
                pltpu.VMEM((ch_b // 128, n_out_row * w_out * 17 + 7, 128), F32),
                pltpu.VMEM((n_out_row, n_img, w_out, ch_b), BF16),
                pltpu.VMEM((12 * ch_a, ch_b), BF16),
                pltpu.VMEM((9 * ch_a, ch_b), BF16),
                pltpu.VMEM((n_layers_b, 9 * ch_b, ch_b), BF16),
                pltpu.VMEM((n_stats, 2, ch_b), F32),
                pltpu.VMEM((n_stats, n_group, 2, ch_b), F32),
                dma((n_row,)), dma((28,)), dma((3,)), dma((3,)),
                dma((n_stats, n_group)), dma((n_stats, n_group)),
                dma((n_layers_b, 2)), dma((n_layers_b, 2)), dma((n_out_row,)),
            ],
            compiler_params=pltpu.CompilerParams(
                collective_id=0, has_side_effects=True, vmem_limit_bytes=67043328),
        )(img, w_a[0], norm_a, w_down, norm_down, w_b.reshape(n_layers_b, 9 * ch_b, ch_b), norm_b)

    act_spec = P(('pod', 'dp'), 'sp', None, None)
    return jax.shard_map(local_stack, mesh=mesh, in_specs=(act_spec, P(), P(), P(), P(), P(), P()), out_specs=act_spec, check_vma=False)
```

time: 294 us -> 101 us (0.34)
  blocking collectives: 181 us -> 0 us
  Pallas kernels: 0 us -> 96.4 us
  matrix products: 52 us -> 0 us
  other arithmetic: 21 us -> 0 us
  waiting for transfers between devices: 15.5 us -> 0 us
  starting transfers between devices: 13.1 us -> 0 us
  local copies, waits for them, and re-layouts: 10.5 us -> 4.41 us
    psum x5 -> x0, blocking collectives: 181 us -> none  [batch_norm(): group_sums = lax.psum(local_sums, ('dp', 'sp'))]
    pallas_call x0 -> x1, Pallas kernels: none -> 96.4 us  [local_stack(): pl.pallas_call(functools.partial(stack_kernel, n_dp, n_sp), out_shape=jax...]
    conv_general_dilated x5 -> x0, matrix products: 52 us -> none  [the longest x4 46.4 us: same_layer(): lax.conv_general_dilated(padded, weight, (1, 1), ((0, 0), (1, 1)), dimens...]
    convert_element_type x5 -> x0, other arithmetic: 20.8 us -> none  [batch_norm(): return jnp.maximum(scaled, 0.0).astype(jnp.bfloat16)]
    ppermute x9 -> x0, waiting for transfers between devices: 15.5 us -> none  [the longest x4 11.4 us: same_layer(): bottom_rows = lax.ppermute(hidden[:, :1], 'sp', to_upper)]
    ppermute x9 -> x0, starting transfers between devices: 13.1 us -> none  [the longest x4 6.47 us: same_layer(): top_rows = lax.ppermute(hidden[:, -1:], 'sp', to_lower)]
    unnamed x13 -> x0, local copies, waits for them, and re-layouts: 6.21 us -> none
    pallas_call x0 -> x1, local copies, waits for them, and re-layouts: none -> 4.41 us  [local_stack(): pl.pallas_call(functools.partial(stack_kernel, n_dp, n_sp), out_shape=jax...]
  transfers between devices with their start and end apart: 9 -> 0, of which waited for: 9 -> 0; matrix products, arithmetic and copies ran while one was open for 0% -> 0% of each run, Pallas kernels for 0% -> 0%
where the time goes in v1:
time: 101 us
  Pallas kernels  96.4 us (95%)
  local copies, waits for them, and re-layouts  4.41 us (4%)
    pallas_call x1, Pallas kernels, local_stack(): pl.pallas_call(functools.partial(stack_kernel, n_dp, n_sp), out_shape=jax...  96.4 us
    pallas_call x1, local copies, waits for them, and re-layouts, local_stack(): pl.pallas_call(functools.partial(stack_kernel, n_dp, n_sp), out_shape=jax...  4.41 us

profile of v1, /device:TPU:0, one launch (start us, length us, event | category | flops | bytes accessed | tf_op | source)
XLA Modules:
  0.0 100.9 jit_solution(2648711505205443553)
XLA Ops:
  0.0 96.4 %shard_map.73 = bf16[16,4,84,256]{3,2,1,0:T(8,128)(2,1)} custom-call(bf16[16,8,168,128]{3,2,1,0:T(8,128)(2,1)} %img.1, bf16[3,3,128,128]{3,2,1,0:T(8,128)(2,1)} %bitcast.3, f32[1,2,128]{2,1,0:T(2,128)} %na.1, bf16[3,3,128,256]{3,2,1,0:T(8,128)(2,1)} %wd.1, f32[2,256]{1,0:T(2,128)} %nd.1, bf16[3,2304,256]{2,1,0:T(8,128)(2,1)} %bitcast.2, f32[3,2,256]{2,1,0:T(2,128)} %nb.1), custom_call_target="tpu_custom_call" | custom-call | tf_op jit(solution)/shard_map/pallas_call | solution.py:324
  96.5 4.4 %copy.8 = bf16[16,4,84,256]{3,1,2,0:T(4,128)(2,1)} copy(bf16[16,4,84,256]{3,2,1,0:T(8,128)(2,1)} %shard_map.73) | data formatting | bytes 5505024 | tf_op jit(solution)/shard_map/pallas_call | solution.py:324

commit v2 on v1

--- a/solution.py
+++ b/solution.py
@@ -13,11 +13,11 @@
 F32 = jnp.float32
 
 
-def stack_kernel(n_dp, n_sp, img, wa, na, wd, nd, wb, nb, out,
-                 nat, stage, img_t, act_a, act_b, zbuf, zfin, out_nat,
+def stack_kernel(n_dp, n_sp, n_early, img, wa, na, wd, nd, wb, nb, out,
+                 nat, stage, img_t, act_a, act_b, zbuf, zhalo, zfin, out_nat,
                  wa_v, wd_v, wb_v, stat_src, stat_dst,
                  in_sem, w_sem, halo_in_send, halo_in_recv, stat_send, stat_recv,
-                 halo_send, halo_recv, out_sem):
+                 halo_send, halo_recv, early_send, early_recv, out_sem):
     n_img, n_row, width, ch_a = img.shape
     n_out_row, w_out, ch_b = out.shape[1], out.shape[2], out.shape[3]
     n_layers_b = wb.shape[0]
@@ -80,8 +80,6 @@
         nat[n_row + 2] = jnp.zeros((n_img, width, ch_a), BF16)
         act_b[n_out_row + 1] = jnp.zeros((w_out + 2, n_img, ch_b), BF16)
 
-    pl.semaphore_wait(barrier, n_group - 1)
-
     def image_halo(src_row, dst_row, dev, k):
         return pltpu.make_async_remote_copy(
             src_ref=img.at[:, src_row], dst_ref=nat.at[dst_row], send_sem=halo_in_send.at[k],
@@ -90,15 +88,6 @@
     to_lower = image_halo(n_row - 1, 0, lower, 0)
     to_upper0 = image_halo(0, n_row + 1, upper, 1)
     to_upper1 = image_halo(1, n_row + 2, upper, 2)
-
-    @pl.when(not_bottom)
-    def _():
-        to_lower.start()
-
-    @pl.when(not_top)
-    def _():
-        to_upper0.start()
-        to_upper1.start()
 
     def transpose_row(k):
         pitch = stage.shape[0] // n_img
@@ -114,35 +103,26 @@
         z3 = z_val.reshape(m_row // 8, 8, ch_b)
         return total[0] + jnp.sum(z3, axis=0), total[1] + jnp.sum(z3 * z3, axis=0)
 
-    def conv_a(r):
+    def conv_a(r, rows=(0, 1, 2)):
         parts = []
-        for p in range(3):
+        for p in rows:
             for k in range(2):
                 parts.append(img_t[r + p, pl.ds(k, w_out)].reshape(m_row, 2 * ch_a))
-        return jnp.dot(jnp.concatenate(parts, axis=1), wa_v[...], preferred_element_type=F32)
+        w_val = wa_v[pl.ds(rows[0] * 4 * ch_a, len(rows) * 4 * ch_a)]
+        return jnp.dot(jnp.concatenate(parts, axis=1), w_val, preferred_element_type=F32)
 
     def conv_down(r):
         parts = [act_a[2 * r + p, pl.ds(0, w_out)].reshape(m_row, 2 * ch_a) for p in range(3)]
         parts += [act_a[2 * r + p, pl.ds(1, w_out), :, 0:ch_a].reshape(m_row, ch_a) for p in range(3)]
         return jnp.dot(jnp.concatenate(parts, axis=1), wd_v[...], preferred_element_type=F32)
 
-    def conv_b(r, layer):
+    def conv_b(r, layer, rows=(0, 1, 2)):
         parts = []
-        for p in range(3):
+        for p in rows:
             for q in range(3):
                 parts.append(act_b[r + p, pl.ds(q, w_out)].reshape(m_row, ch_b))
-        return jnp.dot(jnp.concatenate(parts, axis=1), wb_v[layer], preferred_element_type=F32)
-
-    def run_rows(rows, conv, total, keep):
-        first, step, count = rows
-
-        def body(i, total):
-            r = first + i * step
-            z_val = conv(r)
-            keep(r, z_val)
-            return fold(total, z_val)
-
-        return lax.fori_loop(0, count, body, total)
+        w_val = wb_v[layer, pl.ds(rows[0] * 3 * ch_b, len(rows) * 3 * ch_b)]
+        return jnp.dot(jnp.concatenate(parts, axis=1), w_val, preferred_element_type=F32)
 
     def keep_z(r, z_val):
         zbuf[r] = z_val
@@ -174,8 +154,9 @@
         return copies
 
     def finish_stats(layer, copies, gamma, beta, count):
-        for c in copies:
-            c.wait()
+        with jax.named_scope("stats_wait"):
+            for c in copies:
+                c.wait()
         tot = jnp.sum(stat_dst[layer], axis=0)
         mean = tot[0:1] / count
         var = tot[1:2] / count - mean * mean
@@ -188,99 +169,188 @@
 
     zeros = (jnp.zeros((8, ch_b), F32), jnp.zeros((8, ch_b), F32))
 
-    for c in row_copies:
-        c.wait()
-
-    def t_body(k, carry):
-        transpose_row(k)
+    def t_body(r, carry):
+        pltpu.make_async_copy(img.at[:, r], nat.at[r + 1], in_sem.at[r]).wait()
+        transpose_row(r + 1)
         return carry
 
-    lax.fori_loop(1, n_row + 1, t_body, 0)
+    with jax.named_scope("transpose"):
+        lax.fori_loop(0, n_row, t_body, 0)
+    with jax.named_scope("barrier"):
+        pl.semaphore_wait(barrier, n_group - 1)
+
+    @pl.when(not_bottom)
+    def _():
+        to_lower.start()
+
+    @pl.when(not_top)
+    def _():
+        to_upper0.start()
+        to_upper1.start()
+
     for c in w_copies:
         c.wait()
-    total = run_rows((1, 1, n_row - 2), conv_a, zeros, keep_z)
-
-    @pl.when(not_top)
-    def _():
-        to_lower.wait_recv()
-
-    @pl.when(not_bottom)
-    def _():
-        to_upper0.wait_recv()
-        to_upper1.wait_recv()
-
-    def t_body_halo(k, carry):
-        transpose_row(jnp.where(k == 0, 0, n_row + k))
-        return carry
-
-    lax.fori_loop(0, 3, t_body_halo, 0)
-    total = run_rows((0, n_row - 1, 2), conv_a, total, keep_z)
-    copies = send_stats(0, total)
-    zbuf[n_row] = conv_a(n_row)
+
+    def a_body(i, total):
+        r = 1 + 2 * i
+        z_pair = [conv_a(r), conv_a(r + 1)]
+        for j in range(2):
+            keep_z(r + j, z_pair[j])
+            total = fold(total, z_pair[j])
+        return total
+
+    with jax.named_scope("conv_a"):
+        total = lax.fori_loop(0, (n_row - 2) // 2, a_body, zeros)
+    with jax.named_scope("conv_a_part"):
+        keep_z(0, conv_a(0, (1, 2)))
+        keep_z(n_row - 1, conv_a(n_row - 1, (0, 1)))
+    with jax.named_scope("img_halo_wait"):
+        @pl.when(not_top)
+        def _():
+            to_lower.wait_recv()
+
+        @pl.when(not_bottom)
+        def _():
+            to_upper0.wait_recv()
+
+    with jax.named_scope("transpose_halo"):
+        transpose_row(0)
+        transpose_row(n_row + 1)
+    with jax.named_scope("conv_a_edge"):
+        for r, p in ((0, 0), (n_row - 1, 2)):
+            z_val = conv_a(r, (p,)) + zbuf[r]
+            keep_z(r, z_val)
+            total = fold(total, z_val)
+    with jax.named_scope("send_stats"):
+        copies = send_stats(0, total)
+    with jax.named_scope("img_halo_wait2"):
+        @pl.when(not_bottom)
+        def _():
+            to_upper1.wait_recv()
+
+    with jax.named_scope("conv_a_extra"):
+        transpose_row(n_row + 2)
+        zbuf[n_row] = conv_a(n_row)
     n_a = float(n_group * n_img * n_row * width)
     wide = lambda v: jnp.concatenate([v, v], axis=1)
-    coef = finish_stats(0, copies, wide(na[0, 0:1]), wide(na[0, 1:2]), n_a)
-
-    def norm_a_body(r, carry):
-        act_a[r, pl.ds(0, w_out)] = normalize(zbuf[r], coef).reshape(w_out, n_img, 2 * ch_a)
-        return carry
-
-    lax.fori_loop(0, n_row + 1, norm_a_body, 0)
-
-    @pl.when(is_bottom)
-    def _():
-        act_a[n_row] = jnp.zeros((w_out + 1, n_img, 2 * ch_a), BF16)
-
-    total = run_rows((0, 1, n_out_row), conv_down, zeros, keep_z)
-    copies = send_stats(1, total)
-    n_b = float(n_group * m_row * n_out_row)
-    coef = finish_stats(1, copies, nd[0:1], nd[1:2], n_b)
-
-    for layer in range(n_layers_b):
-        def norm_b_row(r):
-            act_b[r + 1, pl.ds(1, w_out)] = normalize(zbuf[r], coef).reshape(w_out, n_img, ch_b)
-
+    coef_a = finish_stats(0, copies, wide(na[0, 0:1]), wide(na[0, 1:2]), n_a)
+
+    def norm_a_row(r):
+        y_val = normalize(zbuf[r], coef_a)
+        if r == n_row:
+            y_val = jnp.where(is_bottom, jnp.zeros_like(y_val), y_val)
+        act_a[r, pl.ds(0, w_out)] = y_val.reshape(w_out, n_img, 2 * ch_a)
+
+    with jax.named_scope("conv_down"):
+        total = zeros
+        norm_a_row(0)
+        for r in range(n_out_row):
+            norm_a_row(2 * r + 1)
+            norm_a_row(2 * r + 2)
+            z_val = conv_down(r)
+            zbuf[2 * r] = z_val
+            total = fold(total, z_val)
+
+    n_late = w_out - n_early
+    last_row = n_out_row - 1
+
+    def z_row(layer, r):
+        return 2 * r if layer == 0 else r
+
+    def early_copies(layer):
+        slot = layer % 2
+        up = pltpu.make_async_remote_copy(
+            src_ref=zbuf.at[z_row(layer, 0), pl.ds(0, n_early * n_img)], dst_ref=zhalo.at[slot, 1], send_sem=early_send.at[layer, 1],
+            recv_sem=early_recv.at[layer, 1], device_id=upper, device_id_type=MESH)
         down = pltpu.make_async_remote_copy(
-            src_ref=act_b.at[n_out_row, pl.ds(1, w_out)], dst_ref=act_b.at[0, pl.ds(1, w_out)],
+            src_ref=zbuf.at[z_row(layer, last_row), pl.ds(0, n_early * n_img)], dst_ref=zhalo.at[slot, 0], send_sem=early_send.at[layer, 0],
+            recv_sem=early_recv.at[layer, 0], device_id=lower, device_id_type=MESH)
+        return up, down
+
+    def late_copies(layer):
+        cols = pl.ds(1 + n_early, n_late)
+        up = pltpu.make_async_remote_copy(
+            src_ref=act_b.at[1, cols], dst_ref=act_b.at[n_out_row + 1, cols],
+            send_sem=halo_send.at[layer, 1], recv_sem=halo_recv.at[layer, 1], device_id=upper, device_id_type=MESH)
+        down = pltpu.make_async_remote_copy(
+            src_ref=act_b.at[n_out_row, cols], dst_ref=act_b.at[0, cols],
             send_sem=halo_send.at[layer, 0], recv_sem=halo_recv.at[layer, 0], device_id=lower, device_id_type=MESH)
-        up = pltpu.make_async_remote_copy(
-            src_ref=act_b.at[1, pl.ds(1, w_out)], dst_ref=act_b.at[n_out_row + 1, pl.ds(1, w_out)],
-            send_sem=halo_send.at[layer, 1], recv_sem=halo_recv.at[layer, 1], device_id=upper, device_id_type=MESH)
-
-        norm_b_row(0)
-
+        return up, down
+
+    def start_both(up, down):
         @pl.when(not_top)
         def _():
             up.start()
 
-        norm_b_row(n_out_row - 1)
-
         @pl.when(not_bottom)
         def _():
             down.start()
 
-        def norm_b_body(r, carry):
-            norm_b_row(r)
-            return carry
-
-        lax.fori_loop(1, n_out_row - 1, norm_b_body, 0)
+    n_b = float(n_group * m_row * n_out_row)
+    with jax.named_scope("send_stats"):
+        copies = send_stats(1, total)
+        up_early, down_early = early_copies(0)
+        start_both(up_early, down_early)
+    coef = finish_stats(1, copies, nd[0:1], nd[1:2], n_b)
+
+    for layer in range(n_layers_b):
+        def norm_b_cols(r, first, count):
+            z_val = zbuf[z_row(layer, r), pl.ds(first * n_img, count * n_img)]
+            act_b[r + 1, pl.ds(1 + first, count)] = normalize(z_val, coef).reshape(count, n_img, ch_b)
+
+        up, down = late_copies(layer)
+        with jax.named_scope("norm_edge"):
+            norm_b_cols(0, n_early, n_late)
+            norm_b_cols(last_row, n_early, n_late)
+            start_both(up, down)
+
         last = layer == n_layers_b - 1
-        conv = functools.partial(conv_b, layer=layer)
         keep = keep_final if last else keep_z
-        total = run_rows((1, 1, n_out_row - 2), conv, zeros, keep)
-
-        @pl.when(not_top)
-        def _():
-            up.wait_send()
-            down.wait_recv()
-
-        @pl.when(not_bottom)
-        def _():
-            down.wait_send()
-            up.wait_recv()
-
-        total = run_rows((0, n_out_row - 1, 2), conv, total, keep)
-        copies = send_stats(2 + layer, total)
+        with jax.named_scope("conv_b_main"):
+            norm_b_cols(0, 0, n_early)
+            norm_b_cols(last_row, 0, n_early)
+            for r in range(1, last_row):
+                norm_b_cols(r, 0, w_out)
+            total = zeros
+            zbuf[n_row - 1] = conv_b(0, layer, (1, 2))
+            for r in range(1, last_row):
+                z_val = conv_b(r, layer)
+                keep(r, z_val)
+                total = fold(total, z_val)
+            zbuf[n_row] = conv_b(last_row, layer, (0, 1))
+
+        with jax.named_scope("halo_wait"):
+            def norm_halo(side, row):
+                y_val = normalize(zhalo[layer % 2, side], coef)
+                act_b[row, pl.ds(1, n_early)] = y_val.reshape(n_early, n_img, ch_b)
+
+            @pl.when(not_top)
+            def _():
+                up_early.wait_send()
+                down_early.wait_recv()
+                norm_halo(0, 0)
+                up.wait_send()
+                down.wait_recv()
+
+            @pl.when(not_bottom)
+            def _():
+                down_early.wait_send()
+                up_early.wait_recv()
+                norm_halo(1, n_out_row + 1)
+                down.wait_send()
+                up.wait_recv()
+
+        with jax.named_scope("conv_b_edge"):
+            for j, r, p in ((0, 0, 0), (1, last_row, 2)):
+                z_val = conv_b(r, layer, (p,)) + zbuf[n_row - 1 + j]
+                keep(r, z_val)
+                total = fold(total, z_val)
+
+        with jax.named_scope("send_stats"):
+            copies = send_stats(2 + layer, total)
+            if not last:
+                up_early, down_early = early_copies(layer + 1)
+                start_both(up_early, down_early)
         coef = finish_stats(2 + layer, copies, nb[layer, 0:1], nb[layer, 1:2], n_b)
 
     pitch = zfin.shape[1] // (n_out_row * w_out)
@@ -294,7 +364,8 @@
         pltpu.make_async_copy(out_nat.at[r], out.at[:, r], out_sem.at[r]).start()
         return carry
 
-    lax.fori_loop(0, n_out_row, out_body, 0)
+    with jax.named_scope("final_norm"):
+        lax.fori_loop(0, n_out_row, out_body, 0)
     for r in range(n_out_row):
         pltpu.make_async_copy(out_nat.at[r], out.at[:, r], out_sem.at[r]).wait()
 
@@ -321,8 +392,9 @@
         vmem_spec = pl.BlockSpec(memory_space=pltpu.VMEM)
         dma = pltpu.SemaphoreType.DMA
         n_stats = 2 + n_layers_b
+        n_early = w_out // 3
         return pl.pallas_call(
-            functools.partial(stack_kernel, n_dp, n_sp),
+            functools.partial(stack_kernel, n_dp, n_sp, n_early),
             out_shape=jax.ShapeDtypeStruct((n_img, n_out_row, w_out, ch_b), BF16),
             in_specs=[any_spec, any_spec, vmem_spec, any_spec, vmem_spec, any_spec, vmem_spec],
             out_specs=any_spec,
@@ -333,6 +405,7 @@
                 pltpu.VMEM((n_row + 1, w_out + 1, n_img, 2 * ch_a), BF16),
                 pltpu.VMEM((n_out_row + 2, w_out + 2, n_img, ch_b), BF16),
                 pltpu.VMEM((n_row + 1, w_out * n_img, ch_b), F32),
+                pltpu.VMEM((2, 2, n_early * n_img, ch_b), F32),
                 pltpu.VMEM((ch_b // 128, n_out_row * w_out * 17 + 7, 128), F32),
                 pltpu.VMEM((n_out_row, n_img, w_out, ch_b), BF16),
                 pltpu.VMEM((12 * ch_a, ch_b), BF16),
@@ -342,7 +415,7 @@
                 pltpu.VMEM((n_stats, n_group, 2, ch_b), F32),
                 dma((n_row,)), dma((28,)), dma((3,)), dma((3,)),
                 dma((n_stats, n_group)), dma((n_stats, n_group)),
-                dma((n_layers_b, 2)), dma((n_layers_b, 2)), dma((n_out_row,)),
+                dma((n_layers_b, 2)), dma((n_layers_b, 2)), dma((n_layers_b, 2)), dma((n_layers_b, 2)), dma((n_out_row,)),
             ],
             compiler_params=pltpu.CompilerParams(
                 collective_id=0, has_side_effects=True, vmem_limit_bytes=67043328),

time: 101 us -> 88.5 us (0.88)
  Pallas kernels: 96.4 us -> 83.9 us
    pallas_call x1, Pallas kernels: 96.4 us -> 83.9 us  [local_stack(): pl.pallas_call(functools.partial(stack_kernel, n_dp, n_sp, n_early), out_...]
where the time goes in v2:
time: 88.5 us; the launch traced here: 88.3 us
  Pallas kernels  83.9 us (95%)
  local copies, waits for them, and re-layouts  4.41 us (5%)
    pallas_call x1, Pallas kernels, local_stack(): pl.pallas_call(functools.partial(stack_kernel, n_dp, n_sp, n_early), out_...  83.9 us
    pallas_call x1, local copies, waits for them, and re-layouts, local_stack(): pl.pallas_call(functools.partial(stack_kernel, n_dp, n_sp, n_early), out_...  4.41 us

profile of v2, /device:TPU:0, one launch (start us, length us, event | category | flops | bytes accessed | tf_op | source)
XLA Modules:
  0.0 88.3 jit_solution(1488366416925759760)
XLA Ops:
  0.0 83.9 %shard_map.73 = bf16[16,4,84,256]{3,2,1,0:T(8,128)(2,1)} custom-call(bf16[16,8,168,128]{3,2,1,0:T(8,128)(2,1)} %img.1, bf16[3,3,128,128]{3,2,1,0:T(8,128)(2,1)} %bitcast.3, f32[1,2,128]{2,1,0:T(2,128)} %na.1, bf16[3,3,128,256]{3,2,1,0:T(8,128)(2,1)} %wd.1, f32[2,256]{1,0:T(2,128)} %nd.1, bf16[3,2304,256]{2,1,0:T(8,128)(2,1)} %bitcast.2, f32[3,2,256]{2,1,0:T(2,128)} %nb.1), custom_call_target="tpu_custom_call" | custom-call | tf_op jit(solution)/shard_map/pallas_call | solution.py:396
  83.9 4.4 %copy.8 = bf16[16,4,84,256]{3,1,2,0:T(4,128)(2,1)} copy(bf16[16,4,84,256]{3,2,1,0:T(8,128)(2,1)} %shard_map.73) | data formatting | bytes 5505024 | tf_op jit(solution)/shard_map/pallas_call | solution.py:396

commit v3 on v2

--- a/solution.py
+++ b/solution.py
@@ -13,13 +13,13 @@
 F32 = jnp.float32
 
 
-def stack_kernel(n_dp, n_sp, n_early, img, wa, na, wd, nd, wb, nb, out,
-                 nat, stage, img_t, act_a, act_b, zbuf, zhalo, zfin, out_nat,
+def stack_kernel(n_dp, n_sp, n_early, img, wa, na, wd, nd, wb, nb, z_out, stat_out,
+                 nat, stage, img_t, act_a, act_b, zbuf, zhalo, zfin,
                  wa_v, wd_v, wb_v, stat_src, stat_dst,
                  in_sem, w_sem, halo_in_send, halo_in_recv, stat_send, stat_recv,
-                 halo_send, halo_recv, early_send, early_recv, out_sem):
+                 halo_send, halo_recv, early_send, early_recv, out_sem, own_sem):
     n_img, n_row, width, ch_a = img.shape
-    n_out_row, w_out, ch_b = out.shape[1], out.shape[2], out.shape[3]
+    n_out_row, w_out, ch_b = n_row // 2, width // 2, wd.shape[3]
     n_layers_b = wb.shape[0]
     n_group = n_dp * n_sp
     m_row = w_out * n_img
@@ -87,14 +87,22 @@
 
     to_lower = image_halo(n_row - 1, 0, lower, 0)
     to_upper0 = image_halo(0, n_row + 1, upper, 1)
-    to_upper1 = image_halo(1, n_row + 2, upper, 2)
-
-    def transpose_row(k):
+    cols_x = width * 4 // 7 // 16 * 16
+    n_pair = cols_x // 2 - 1
+    to_upper1 = pltpu.make_async_remote_copy(
+        src_ref=img.at[:, 1, pl.ds(0, cols_x)], dst_ref=nat.at[n_row + 2, :, pl.ds(0, cols_x)], send_sem=halo_in_send.at[2],
+        recv_sem=halo_in_recv.at[2], device_id=upper, device_id_type=MESH)
+    far = pl.ds(n_pair * n_img, (w_out - n_pair) * n_img)
+    to_upper_z = pltpu.make_async_remote_copy(
+        src_ref=zbuf.at[0, far], dst_ref=zbuf.at[n_row, far], send_sem=halo_in_send.at[3],
+        recv_sem=halo_in_recv.at[3], device_id=upper, device_id_type=MESH)
+
+    def transpose_row(k, cols=width):
         pitch = stage.shape[0] // n_img
 
         for i in range(n_img):
-            stage[pl.ds(i * pitch, width), :] = nat[k, i].astype(F32)
-        for x in range(width):
+            stage[pl.ds(i * pitch, cols), :] = nat[k, i, 0:cols].astype(F32)
+        for x in range(cols):
             half = (x + 1) % 2
             img_t[k, (x + 1) // 2, :, half * ch_a:(half + 1) * ch_a] = (
                 stage[pl.ds(x, n_img, stride=pitch), :].astype(BF16))
@@ -103,11 +111,11 @@
         z3 = z_val.reshape(m_row // 8, 8, ch_b)
         return total[0] + jnp.sum(z3, axis=0), total[1] + jnp.sum(z3 * z3, axis=0)
 
-    def conv_a(r, rows=(0, 1, 2)):
+    def conv_a(r, rows=(0, 1, 2), pairs=w_out):
         parts = []
         for p in rows:
             for k in range(2):
-                parts.append(img_t[r + p, pl.ds(k, w_out)].reshape(m_row, 2 * ch_a))
+                parts.append(img_t[r + p, pl.ds(k, pairs)].reshape(pairs * n_img, 2 * ch_a))
         w_val = wa_v[pl.ds(rows[0] * 4 * ch_a, len(rows) * 4 * ch_a)]
         return jnp.dot(jnp.concatenate(parts, axis=1), w_val, preferred_element_type=F32)
 
@@ -128,10 +136,10 @@
         zbuf[r] = z_val
 
     def keep_final(r, z_val):
-        pitch = zfin.shape[1] // (n_out_row * w_out)
         for x in range(w_out):
             for h in range(ch_b // 128):
-                zfin[h, pl.ds((r * w_out + x) * pitch, n_img), :] = z_val[x * n_img:(x + 1) * n_img, h * 128:(h + 1) * 128]
+                zfin[h, pl.ds(x * n_img * n_out_row + r, n_img, stride=n_out_row), :] = (
+                    z_val[x * n_img:(x + 1) * n_img, h * 128:(h + 1) * 128])
 
     def send_stats(layer, total):
         s1 = jnp.sum(total[0], axis=0, keepdims=True)
@@ -143,14 +151,20 @@
             s2 = jnp.concatenate([s2, s2], axis=1)
         both = jnp.concatenate([s1, s2], axis=0)
         stat_src[layer] = both
-        stat_dst[layer, me] = both
+        last = layer == stat_src.shape[0] - 1
+        slot = stat_out.at[me] if last else stat_dst.at[layer, me]
+        if not last:
+            stat_dst[layer, me] = both
         copies = []
         for i in range(1, n_group):
             copies.append(pltpu.make_async_remote_copy(
-                src_ref=stat_src.at[layer], dst_ref=stat_dst.at[layer, me], send_sem=stat_send.at[layer, i],
+                src_ref=stat_src.at[layer], dst_ref=slot, send_sem=stat_send.at[layer, i],
                 recv_sem=stat_recv.at[layer, i], device_id=peer(i), device_id_type=MESH))
         for c in copies:
             c.start()
+        if last:
+            copies.append(pltpu.make_async_copy(stat_src.at[layer], slot, own_sem))
+            copies[-1].start()
         return copies
 
     def finish_stats(layer, copies, gamma, beta, count):
@@ -161,11 +175,14 @@
         mean = tot[0:1] / count
         var = tot[1:2] / count - mean * mean
         scale = gamma * lax.rsqrt(var + EPS_VALUE)
-        return mean, scale, beta
+        return scale, beta - mean * scale
 
     def normalize(z_val, coef):
-        mean, scale, beta = coef
-        return jnp.maximum((z_val - mean) * scale + beta, 0.0).astype(BF16)
+        scale, shift = coef
+        return jnp.maximum(z_val * scale + shift, 0.0).astype(BF16)
+
+    def z_row(layer, r):
+        return 2 * r + (layer + 1) % 2
 
     zeros = (jnp.zeros((8, ch_b), F32), jnp.zeros((8, ch_b), F32))
 
@@ -223,14 +240,19 @@
             total = fold(total, z_val)
     with jax.named_scope("send_stats"):
         copies = send_stats(0, total)
+
+        @pl.when(not_top)
+        def _():
+            to_upper_z.start()
+
     with jax.named_scope("img_halo_wait2"):
         @pl.when(not_bottom)
         def _():
             to_upper1.wait_recv()
 
     with jax.named_scope("conv_a_extra"):
-        transpose_row(n_row + 2)
-        zbuf[n_row] = conv_a(n_row)
+        transpose_row(n_row + 2, cols_x)
+        zbuf[n_row, 0:n_pair * n_img] = conv_a(n_row, pairs=n_pair)
     n_a = float(n_group * n_img * n_row * width)
     wide = lambda v: jnp.concatenate([v, v], axis=1)
     coef_a = finish_stats(0, copies, wide(na[0, 0:1]), wide(na[0, 1:2]), n_a)
@@ -241,21 +263,34 @@
             y_val = jnp.where(is_bottom, jnp.zeros_like(y_val), y_val)
         act_a[r, pl.ds(0, w_out)] = y_val.reshape(w_out, n_img, 2 * ch_a)
 
+    def down_row(r, total):
+        z_val = conv_down(r)
+        zbuf[z_row(0, r)] = z_val
+        return fold(total, z_val)
+
     with jax.named_scope("conv_down"):
         total = zeros
         norm_a_row(0)
-        for r in range(n_out_row):
+        for r in range(n_out_row - 1):
             norm_a_row(2 * r + 1)
             norm_a_row(2 * r + 2)
-            z_val = conv_down(r)
-            zbuf[2 * r] = z_val
-            total = fold(total, z_val)
+            total = down_row(r, total)
+        norm_a_row(n_row - 1)
+    with jax.named_scope("down_halo_wait"):
+        @pl.when(not_top)
+        def _():
+            to_upper_z.wait_send()
+
+        @pl.when(not_bottom)
+        def _():
+            to_upper_z.wait_recv()
+
+    with jax.named_scope("conv_down_last"):
+        norm_a_row(n_row)
+        total = down_row(n_out_row - 1, total)
 
     n_late = w_out - n_early
     last_row = n_out_row - 1
-
-    def z_row(layer, r):
-        return 2 * r if layer == 0 else r
 
     def early_copies(layer):
         slot = layer % 2
@@ -305,19 +340,24 @@
             start_both(up, down)
 
         last = layer == n_layers_b - 1
-        keep = keep_final if last else keep_z
+        def keep(r, z_val):
+            if last:
+                keep_final(r, z_val)
+            else:
+                zbuf[z_row(layer + 1, r)] = z_val
+
         with jax.named_scope("conv_b_main"):
             norm_b_cols(0, 0, n_early)
             norm_b_cols(last_row, 0, n_early)
             for r in range(1, last_row):
                 norm_b_cols(r, 0, w_out)
             total = zeros
-            zbuf[n_row - 1] = conv_b(0, layer, (1, 2))
+            zbuf[z_row(layer + 1, 0)] = conv_b(0, layer, (1, 2))
             for r in range(1, last_row):
                 z_val = conv_b(r, layer)
                 keep(r, z_val)
                 total = fold(total, z_val)
-            zbuf[n_row] = conv_b(last_row, layer, (0, 1))
+            zbuf[z_row(layer + 1, last_row)] = conv_b(last_row, layer, (0, 1))
 
         with jax.named_scope("halo_wait"):
             def norm_halo(side, row):
@@ -341,8 +381,8 @@
                 up.wait_recv()
 
         with jax.named_scope("conv_b_edge"):
-            for j, r, p in ((0, 0, 0), (1, last_row, 2)):
-                z_val = conv_b(r, layer, (p,)) + zbuf[n_row - 1 + j]
+            for r, p in ((0, 0), (last_row, 2)):
+                z_val = conv_b(r, layer, (p,)) + zbuf[z_row(layer + 1, r)]
                 keep(r, z_val)
                 total = fold(total, z_val)
 
@@ -351,23 +391,16 @@
             if not last:
                 up_early, down_early = early_copies(layer + 1)
                 start_both(up_early, down_early)
-        coef = finish_stats(2 + layer, copies, nb[layer, 0:1], nb[layer, 1:2], n_b)
-
-    pitch = zfin.shape[1] // (n_out_row * w_out)
-
-    def out_body(r, carry):
-        for i in range(n_img):
-            for h in range(ch_b // 128):
-                lanes = slice(h * 128, (h + 1) * 128)
-                z_val = zfin[h, pl.ds(r * w_out * pitch + i, w_out, stride=pitch), :]
-                out_nat[r, i, :, lanes] = normalize(z_val, tuple(v[:, lanes] for v in coef))
-        pltpu.make_async_copy(out_nat.at[r], out.at[:, r], out_sem.at[r]).start()
-        return carry
-
-    with jax.named_scope("final_norm"):
-        lax.fori_loop(0, n_out_row, out_body, 0)
-    for r in range(n_out_row):
-        pltpu.make_async_copy(out_nat.at[r], out.at[:, r], out_sem.at[r]).wait()
+        if not last:
+            coef = finish_stats(2 + layer, copies, nb[layer, 0:1], nb[layer, 1:2], n_b)
+
+    with jax.named_scope("z_out"):
+        z_copy = pltpu.make_async_copy(zfin, z_out, out_sem)
+        z_copy.start()
+        z_copy.wait()
+    with jax.named_scope("last_stats_wait"):
+        for c in copies:
+            c.wait()
 
     @pl.when(not_bottom)
     def _():
@@ -377,6 +410,52 @@
     def _():
         to_upper0.wait_send()
         to_upper1.wait_send()
+
+
+def finish_kernel(count, z_hbm, stat_hbm, norm_hbm, out, z_v, stat, norms, out_v, z_sem, small_sem, out_sem):
+    n_img, w_out, n_out_row, ch_b = out.shape
+    n_chunk = z_sem.shape[0]
+    chunk = w_out // n_chunk
+    per_col = n_img * n_out_row
+
+    def z_copy(k):
+        rows = pl.ds(k * chunk * per_col, chunk * per_col)
+        return pltpu.make_async_copy(z_hbm.at[:, rows], z_v.at[:, rows], z_sem.at[k])
+
+    def out_copies(k):
+        cols = pl.ds(k * chunk, chunk)
+        return [pltpu.make_async_copy(out_v.at[cols, i], out.at[i, cols], out_sem.at[i, k]) for i in range(n_img)]
+
+    small = [pltpu.make_async_copy(stat_hbm, stat, small_sem.at[0]), pltpu.make_async_copy(norm_hbm, norms, small_sem.at[1])]
+    for c in small:
+        c.start()
+    for k in range(n_chunk):
+        z_copy(k).start()
+    for c in small:
+        c.wait()
+    norm = norms[norms.shape[0] - 1]
+    tot = jnp.sum(stat[...], axis=0)
+    mean = tot[0:1] / count
+    var = tot[1:2] / count - mean * mean
+    scale = norm[0:1] * lax.rsqrt(var + EPS_VALUE)
+    shift = norm[1:2] - mean * scale
+    for k in range(n_chunk):
+        z_copy(k).wait()
+
+        def out_body(x, carry):
+            for h in range(ch_b // 128):
+                lanes = slice(h * 128, (h + 1) * 128)
+                z_val = z_v[h, pl.ds(x * per_col, per_col), :]
+                y_val = jnp.maximum(z_val * scale[:, lanes] + shift[:, lanes], 0.0).astype(BF16)
+                out_v[x, :, :, lanes] = y_val.reshape(n_img, n_out_row, 128)
+            return carry
+
+        lax.fori_loop(k * chunk, (k + 1) * chunk, out_body, 0, unroll=3)
+        for c in out_copies(k):
+            c.start()
+    for k in range(n_chunk):
+        for c in out_copies(k):
+            c.wait()
 
 
 def solution(mesh):
@@ -393,11 +472,14 @@
         dma = pltpu.SemaphoreType.DMA
         n_stats = 2 + n_layers_b
         n_early = w_out // 3
-        return pl.pallas_call(
+        z_val, stats = pl.pallas_call(
             functools.partial(stack_kernel, n_dp, n_sp, n_early),
-            out_shape=jax.ShapeDtypeStruct((n_img, n_out_row, w_out, ch_b), BF16),
+            out_shape=(
+                jax.ShapeDtypeStruct((ch_b // 128, n_out_row * w_out * n_img, 128), F32),
+                jax.ShapeDtypeStruct((n_group, 2, ch_b), F32),
+            ),
             in_specs=[any_spec, any_spec, vmem_spec, any_spec, vmem_spec, any_spec, vmem_spec],
-            out_specs=any_spec,
+            out_specs=(any_spec, any_spec),
             scratch_shapes=[
                 pltpu.VMEM((n_row + 3, n_img, width, ch_a), BF16),
                 pltpu.VMEM((n_img * width, 128), F32),
@@ -406,20 +488,34 @@
                 pltpu.VMEM((n_out_row + 2, w_out + 2, n_img, ch_b), BF16),
                 pltpu.VMEM((n_row + 1, w_out * n_img, ch_b), F32),
                 pltpu.VMEM((2, 2, n_early * n_img, ch_b), F32),
-                pltpu.VMEM((ch_b // 128, n_out_row * w_out * 17 + 7, 128), F32),
-                pltpu.VMEM((n_out_row, n_img, w_out, ch_b), BF16),
+                pltpu.VMEM((ch_b // 128, n_out_row * w_out * n_img, 128), F32),
                 pltpu.VMEM((12 * ch_a, ch_b), BF16),
                 pltpu.VMEM((9 * ch_a, ch_b), BF16),
                 pltpu.VMEM((n_layers_b, 9 * ch_b, ch_b), BF16),
                 pltpu.VMEM((n_stats, 2, ch_b), F32),
-                pltpu.VMEM((n_stats, n_group, 2, ch_b), F32),
-                dma((n_row,)), dma((28,)), dma((3,)), dma((3,)),
+                pltpu.VMEM((n_stats - 1, n_group, 2, ch_b), F32),
+                dma((n_row,)), dma((28,)), dma((4,)), dma((4,)),
                 dma((n_stats, n_group)), dma((n_stats, n_group)),
-                dma((n_layers_b, 2)), dma((n_layers_b, 2)), dma((n_layers_b, 2)), dma((n_layers_b, 2)), dma((n_out_row,)),
+                dma((n_layers_b, 2)), dma((n_layers_b, 2)), dma((n_layers_b, 2)), dma((n_layers_b, 2)), dma, dma,
             ],
             compiler_params=pltpu.CompilerParams(
                 collective_id=0, has_side_effects=True, vmem_limit_bytes=67043328),
         )(img, w_a[0], norm_a, w_down, norm_down, w_b.reshape(n_layers_b, 9 * ch_b, ch_b), norm_b)
+        features = pl.pallas_call(
+            functools.partial(finish_kernel, float(n_group * n_img * n_out_row * w_out)),
+            out_shape=jax.ShapeDtypeStruct((n_img, w_out, n_out_row, ch_b), BF16),
+            in_specs=[any_spec, any_spec, any_spec],
+            out_specs=any_spec,
+            scratch_shapes=[
+                pltpu.VMEM(z_val.shape, F32),
+                pltpu.VMEM(stats.shape, F32),
+                pltpu.VMEM(norm_b.shape, F32),
+                pltpu.VMEM((w_out, n_img, n_out_row, ch_b), BF16),
+                dma((4,)), dma((2,)), dma((n_img, 4)),
+            ],
+            compiler_params=pltpu.CompilerParams(vmem_limit_bytes=67043328),
+        )(z_val, stats, norm_b)
+        return features.transpose(0, 2, 1, 3)
 
     act_spec = P(('pod', 'dp'), 'sp', None, None)
     return jax.shard_map(local_stack, mesh=mesh, in_specs=(act_spec, P(), P(), P(), P(), P(), P()), out_specs=act_spec, check_vma=False)

time: 88.5 us -> 84.7 us (0.957)
  local copies, waits for them, and re-layouts: 4.41 us -> 0 us
    pallas_call x0 -> x1, Pallas kernels: none -> 4.81 us  [local_stack(): pl.pallas_call(functools.partial(finish_kernel, float(n_group * n_img * n...]
    pallas_call x1, Pallas kernels: 83.9 us -> 79.5 us  [local_stack(): pl.pallas_call(functools.partial(stack_kernel, n_dp, n_sp, n_early), out_...]
    pallas_call x1 -> x0, local copies, waits for them, and re-layouts: 4.41 us -> none  [local_stack(): pl.pallas_call(functools.partial(stack_kernel, n_dp, n_sp, n_early), out_...]
where the time goes in v3:
time: 84.7 us; the launch traced here: 84.5 us
  Pallas kernels  84.3 us (100%)
    pallas_call x1, Pallas kernels, local_stack(): pl.pallas_call(functools.partial(stack_kernel, n_dp, n_sp, n_early), out_...  79.5 us
    pallas_call x1, Pallas kernels, local_stack(): pl.pallas_call(functools.partial(finish_kernel, float(n_group * n_img * n...  4.81 us

profile of v3, /device:TPU:0, one launch (start us, length us, event | category | flops | bytes accessed | tf_op | source)
XLA Modules:
  0.0 84.5 jit_solution(868491059912720401)
XLA Ops:
  0.0 79.5 %shard_map.73 = (f32[2,5376,128]{2,1,0:T(8,128)}, f32[16,2,256]{2,1,0:T(2,128)}) custom-call(bf16[16,8,168,128]{3,2,1,0:T(8,128)(2,1)} %img.1, bf16[3,3,128,128]{3,2,1,0:T(8,128)(2,1)} %bitcast.4, f32[1,2,128]{2,1,0:T(2,128)} %na.1, bf16[3,3,128,256]{3,2,1,0:T(8,128)(2,1)} %wd.1, f32[2,256]{1,0:T(2,128)} %nd.1, bf16[3,2304,256]{2,1,0:T(8,128)(2,1)} %bitcast.3, ...), custom_call_target="tpu_custom_call" | custom-call | tf_op jit(solution)/shard_map/pallas_call | solution.py:475
  79.5 4.8 %shard_map.74 = bf16[16,84,4,256]{3,2,1,0:T(4,128)(2,1)} custom-call(f32[2,5376,128]{2,1,0:T(8,128)} %get-tuple-element.7.z_hbm, f32[16,2,256]{2,1,0:T(2,128)} %get-tuple-element.8.stat_hbm, f32[3,2,256]{2,1,0:T(2,128)} %norm_hbm.1), custom_call_target="tpu_custom_call" | custom-call | tf_op jit(solution)/shard_map/pallas_call | solution.py:504

commit v4 on v3

--- a/solution.py
+++ b/solution.py
@@ -108,7 +108,7 @@
                 stage[pl.ds(x, n_img, stride=pitch), :].astype(BF16))
 
     def fold(total, z_val):
-        z3 = z_val.reshape(m_row // 8, 8, ch_b)
+        z3 = z_val.reshape(z_val.shape[0] // 8, 8, ch_b)
         return total[0] + jnp.sum(z3, axis=0), total[1] + jnp.sum(z3 * z3, axis=0)
 
     def conv_a(r, rows=(0, 1, 2), pairs=w_out):
@@ -119,26 +119,27 @@
         w_val = wa_v[pl.ds(rows[0] * 4 * ch_a, len(rows) * 4 * ch_a)]
         return jnp.dot(jnp.concatenate(parts, axis=1), w_val, preferred_element_type=F32)
 
-    def conv_down(r):
-        parts = [act_a[2 * r + p, pl.ds(0, w_out)].reshape(m_row, 2 * ch_a) for p in range(3)]
-        parts += [act_a[2 * r + p, pl.ds(1, w_out), :, 0:ch_a].reshape(m_row, ch_a) for p in range(3)]
+    def conv_down(r, first, count):
+        m_val = count * n_img
+        parts = [act_a[2 * r + p, pl.ds(first, count)].reshape(m_val, 2 * ch_a) for p in range(3)]
+        parts += [act_a[2 * r + p, pl.ds(first + 1, count), :, 0:ch_a].reshape(m_val, ch_a) for p in range(3)]
         return jnp.dot(jnp.concatenate(parts, axis=1), wd_v[...], preferred_element_type=F32)
 
-    def conv_b(r, layer, rows=(0, 1, 2)):
+    def conv_b(r, layer, rows=(0, 1, 2), first=0, count=w_out):
         parts = []
         for p in rows:
             for q in range(3):
-                parts.append(act_b[r + p, pl.ds(q, w_out)].reshape(m_row, ch_b))
+                parts.append(act_b[r + p, pl.ds(q + first, count)].reshape(count * n_img, ch_b))
         w_val = wb_v[layer, pl.ds(rows[0] * 3 * ch_b, len(rows) * 3 * ch_b)]
         return jnp.dot(jnp.concatenate(parts, axis=1), w_val, preferred_element_type=F32)
 
     def keep_z(r, z_val):
         zbuf[r] = z_val
 
-    def keep_final(r, z_val):
-        for x in range(w_out):
+    def keep_final(r, z_val, first=0):
+        for x in range(z_val.shape[0] // n_img):
             for h in range(ch_b // 128):
-                zfin[h, pl.ds(x * n_img * n_out_row + r, n_img, stride=n_out_row), :] = (
+                zfin[h, pl.ds((first + x) * n_img * n_out_row + r, n_img, stride=n_out_row), :] = (
                     z_val[x * n_img:(x + 1) * n_img, h * 128:(h + 1) * 128])
 
     def send_stats(layer, total):
@@ -217,8 +218,9 @@
         return total
 
     with jax.named_scope("conv_a"):
-        total = lax.fori_loop(0, (n_row - 2) // 2, a_body, zeros)
+        total = lax.fori_loop(0, (n_row - 4) // 2, a_body, zeros)
     with jax.named_scope("conv_a_part"):
+        total = a_body((n_row - 4) // 2, total)
         keep_z(0, conv_a(0, (1, 2)))
         keep_z(n_row - 1, conv_a(n_row - 1, (0, 1)))
     with jax.named_scope("img_halo_wait"):
@@ -257,25 +259,34 @@
     wide = lambda v: jnp.concatenate([v, v], axis=1)
     coef_a = finish_stats(0, copies, wide(na[0, 0:1]), wide(na[0, 1:2]), n_a)
 
-    def norm_a_row(r):
-        y_val = normalize(zbuf[r], coef_a)
+    n_piece = 3
+    piece = w_out // n_piece
+
+    def norm_a_cols(r, k):
+        y_val = normalize(zbuf[r, k * piece * n_img:(k + 1) * piece * n_img], coef_a)
         if r == n_row:
             y_val = jnp.where(is_bottom, jnp.zeros_like(y_val), y_val)
-        act_a[r, pl.ds(0, w_out)] = y_val.reshape(w_out, n_img, 2 * ch_a)
-
-    def down_row(r, total):
-        z_val = conv_down(r)
-        zbuf[z_row(0, r)] = z_val
+        act_a[r, pl.ds(k * piece, piece)] = y_val.reshape(piece, n_img, 2 * ch_a)
+
+    def norm_a_row(r):
+        for k in range(n_piece):
+            norm_a_cols(r, k)
+
+    def down_cols(r, k, total):
+        z_val = conv_down(r, k * piece, piece)
+        zbuf[z_row(0, r), k * piece * n_img:(k + 1) * piece * n_img] = z_val
         return fold(total, z_val)
 
     with jax.named_scope("conv_down"):
         total = zeros
-        norm_a_row(0)
+        for r in range(3):
+            norm_a_row(r)
         for r in range(n_out_row - 1):
-            norm_a_row(2 * r + 1)
-            norm_a_row(2 * r + 2)
-            total = down_row(r, total)
-        norm_a_row(n_row - 1)
+            for k in range(n_piece):
+                norm_a_cols(2 * r + 3, k)
+                if 2 * r + 4 < n_row:
+                    norm_a_cols(2 * r + 4, k)
+                total = down_cols(r, k, total)
     with jax.named_scope("down_halo_wait"):
         @pl.when(not_top)
         def _():
@@ -287,9 +298,10 @@
 
     with jax.named_scope("conv_down_last"):
         norm_a_row(n_row)
-        total = down_row(n_out_row - 1, total)
-
-    n_late = w_out - n_early
+        for k in range(n_piece):
+            total = down_cols(n_out_row - 1, k, total)
+
+    late_cols = (n_early, (n_early + w_out) // 2, w_out)
     last_row = n_out_row - 1
 
     def early_copies(layer):
@@ -302,14 +314,14 @@
             recv_sem=early_recv.at[layer, 0], device_id=lower, device_id_type=MESH)
         return up, down
 
-    def late_copies(layer):
-        cols = pl.ds(1 + n_early, n_late)
+    def late_copies(layer, k):
+        cols = pl.ds(1 + late_cols[k], late_cols[k + 1] - late_cols[k])
         up = pltpu.make_async_remote_copy(
             src_ref=act_b.at[1, cols], dst_ref=act_b.at[n_out_row + 1, cols],
-            send_sem=halo_send.at[layer, 1], recv_sem=halo_recv.at[layer, 1], device_id=upper, device_id_type=MESH)
+            send_sem=halo_send.at[layer, k, 1], recv_sem=halo_recv.at[layer, k, 1], device_id=upper, device_id_type=MESH)
         down = pltpu.make_async_remote_copy(
             src_ref=act_b.at[n_out_row, cols], dst_ref=act_b.at[0, cols],
-            send_sem=halo_send.at[layer, 0], recv_sem=halo_recv.at[layer, 0], device_id=lower, device_id_type=MESH)
+            send_sem=halo_send.at[layer, k, 0], recv_sem=halo_recv.at[layer, k, 0], device_id=lower, device_id_type=MESH)
         return up, down
 
     def start_both(up, down):
@@ -333,11 +345,12 @@
             z_val = zbuf[z_row(layer, r), pl.ds(first * n_img, count * n_img)]
             act_b[r + 1, pl.ds(1 + first, count)] = normalize(z_val, coef).reshape(count, n_img, ch_b)
 
-        up, down = late_copies(layer)
+        late = [late_copies(layer, k) for k in range(2)]
         with jax.named_scope("norm_edge"):
-            norm_b_cols(0, n_early, n_late)
-            norm_b_cols(last_row, n_early, n_late)
-            start_both(up, down)
+            for k in range(2):
+                norm_b_cols(0, late_cols[k], late_cols[k + 1] - late_cols[k])
+                norm_b_cols(last_row, late_cols[k], late_cols[k + 1] - late_cols[k])
+                start_both(*late[k])
 
         last = layer == n_layers_b - 1
         def keep(r, z_val):
@@ -359,6 +372,20 @@
                 total = fold(total, z_val)
             zbuf[z_row(layer + 1, last_row)] = conv_b(last_row, layer, (0, 1))
 
+        def keep_edge(r, z_val, first):
+            if last:
+                keep_final(r, z_val, first)
+            else:
+                zbuf[z_row(layer + 1, r), first * n_img:first * n_img + z_val.shape[0]] = z_val
+
+        def edge_cols(first, count, total):
+            rows = slice(first * n_img, (first + count) * n_img)
+            for r, p in ((0, 0), (last_row, 2)):
+                z_val = conv_b(r, layer, (p,), first, count) + zbuf[z_row(layer + 1, r), rows]
+                keep_edge(r, z_val, first)
+                total = fold(total, z_val)
+            return total
+
         with jax.named_scope("halo_wait"):
             def norm_halo(side, row):
                 y_val = normalize(zhalo[layer % 2, side], coef)
@@ -369,22 +396,33 @@
                 up_early.wait_send()
                 down_early.wait_recv()
                 norm_halo(0, 0)
-                up.wait_send()
-                down.wait_recv()
+                late[0][0].wait_send()
+                late[0][1].wait_recv()
 
             @pl.when(not_bottom)
             def _():
                 down_early.wait_send()
                 up_early.wait_recv()
                 norm_halo(1, n_out_row + 1)
-                down.wait_send()
-                up.wait_recv()
-
+                late[0][1].wait_send()
+                late[0][0].wait_recv()
+
+        split = late_cols[1] - 1
         with jax.named_scope("conv_b_edge"):
-            for r, p in ((0, 0), (last_row, 2)):
-                z_val = conv_b(r, layer, (p,)) + zbuf[z_row(layer + 1, r)]
-                keep(r, z_val)
-                total = fold(total, z_val)
+            total = edge_cols(0, split, total)
+        with jax.named_scope("halo_wait2"):
+            @pl.when(not_top)
+            def _():
+                late[1][0].wait_send()
+                late[1][1].wait_recv()
+
+            @pl.when(not_bottom)
+            def _():
+                late[1][1].wait_send()
+                late[1][0].wait_recv()
+
+        with jax.named_scope("conv_b_edge2"):
+            total = edge_cols(split, w_out - split, total)
 
         with jax.named_scope("send_stats"):
             copies = send_stats(2 + layer, total)
@@ -422,9 +460,9 @@
         rows = pl.ds(k * chunk * per_col, chunk * per_col)
         return pltpu.make_async_copy(z_hbm.at[:, rows], z_v.at[:, rows], z_sem.at[k])
 
-    def out_copies(k):
+    def out_copy(k):
         cols = pl.ds(k * chunk, chunk)
-        return [pltpu.make_async_copy(out_v.at[cols, i], out.at[i, cols], out_sem.at[i, k]) for i in range(n_img)]
+        return pltpu.make_async_copy(out_v.at[:, cols], out.at[:, cols], out_sem.at[k])
 
     small = [pltpu.make_async_copy(stat_hbm, stat, small_sem.at[0]), pltpu.make_async_copy(norm_hbm, norms, small_sem.at[1])]
     for c in small:
@@ -447,15 +485,13 @@
                 lanes = slice(h * 128, (h + 1) * 128)
                 z_val = z_v[h, pl.ds(x * per_col, per_col), :]
                 y_val = jnp.maximum(z_val * scale[:, lanes] + shift[:, lanes], 0.0).astype(BF16)
-                out_v[x, :, :, lanes] = y_val.reshape(n_img, n_out_row, 128)
+                out_v[:, x, :, lanes] = y_val.reshape(n_img, n_out_row, 128)
             return carry
 
         lax.fori_loop(k * chunk, (k + 1) * chunk, out_body, 0, unroll=3)
-        for c in out_copies(k):
-            c.start()
+        out_copy(k).start()
     for k in range(n_chunk):
-        for c in out_copies(k):
-            c.wait()
+        out_copy(k).wait()
 
 
 def solution(mesh):
@@ -482,7 +518,7 @@
             out_specs=(any_spec, any_spec),
             scratch_shapes=[
                 pltpu.VMEM((n_row + 3, n_img, width, ch_a), BF16),
-                pltpu.VMEM((n_img * width, 128), F32),
+                pltpu.VMEM((n_img * (width + 4), 128), F32),
                 pltpu.VMEM((n_row + 3, w_out + 1, n_img, 2 * ch_a), BF16),
                 pltpu.VMEM((n_row + 1, w_out + 1, n_img, 2 * ch_a), BF16),
                 pltpu.VMEM((n_out_row + 2, w_out + 2, n_img, ch_b), BF16),
@@ -496,11 +532,12 @@
                 pltpu.VMEM((n_stats - 1, n_group, 2, ch_b), F32),
                 dma((n_row,)), dma((28,)), dma((4,)), dma((4,)),
                 dma((n_stats, n_group)), dma((n_stats, n_group)),
-                dma((n_layers_b, 2)), dma((n_layers_b, 2)), dma((n_layers_b, 2)), dma((n_layers_b, 2)), dma, dma,
+                dma((n_layers_b, 2, 2)), dma((n_layers_b, 2, 2)), dma((n_layers_b, 2)), dma((n_layers_b, 2)), dma, dma,
             ],
             compiler_params=pltpu.CompilerParams(
                 collective_id=0, has_side_effects=True, vmem_limit_bytes=67043328),
         )(img, w_a[0], norm_a, w_down, norm_down, w_b.reshape(n_layers_b, 9 * ch_b, ch_b), norm_b)
+        n_chunk = 4
         features = pl.pallas_call(
             functools.partial(finish_kernel, float(n_group * n_img * n_out_row * w_out)),
             out_shape=jax.ShapeDtypeStruct((n_img, w_out, n_out_row, ch_b), BF16),
@@ -510,8 +547,8 @@
                 pltpu.VMEM(z_val.shape, F32),
                 pltpu.VMEM(stats.shape, F32),
                 pltpu.VMEM(norm_b.shape, F32),
-                pltpu.VMEM((w_out, n_img, n_out_row, ch_b), BF16),
-                dma((4,)), dma((2,)), dma((n_img, 4)),
+                pltpu.VMEM((n_img, w_out, n_out_row, ch_b), BF16),
+                dma((n_chunk,)), dma((2,)), dma((n_chunk,)),
             ],
             compiler_params=pltpu.CompilerParams(vmem_limit_bytes=67043328),
         )(z_val, stats, norm_b)

time: 84.7 us -> 79.3 us (0.936)
  Pallas kernels: 84.3 us -> 78.9 us
    pallas_call x1, Pallas kernels: 79.5 us -> 74.6 us  [local_stack(): pl.pallas_call(functools.partial(stack_kernel, n_dp, n_sp, n_early), out_...]
where the time goes in v4:
time: 79.3 us; the launch traced here: 79.1 us
  Pallas kernels  78.9 us (99%)
    pallas_call x1, Pallas kernels, local_stack(): pl.pallas_call(functools.partial(stack_kernel, n_dp, n_sp, n_early), out_...  74.6 us
    pallas_call x1, Pallas kernels, local_stack(): pl.pallas_call(functools.partial(finish_kernel, float(n_group * n_img * n...  4.26 us

profile of v4, /device:TPU:0, one launch (start us, length us, event | category | flops | bytes accessed | tf_op | source)
XLA Modules:
  0.0 79.1 jit_solution(9540118011570634885)
XLA Ops:
  0.0 74.6 %shard_map.73 = (f32[2,5376,128]{2,1,0:T(8,128)}, f32[16,2,256]{2,1,0:T(2,128)}) custom-call(bf16[16,8,168,128]{3,2,1,0:T(8,128)(2,1)} %img.1, bf16[3,3,128,128]{3,2,1,0:T(8,128)(2,1)} %bitcast.4, f32[1,2,128]{2,1,0:T(2,128)} %na.1, bf16[3,3,128,256]{3,2,1,0:T(8,128)(2,1)} %wd.1, f32[2,256]{1,0:T(2,128)} %nd.1, bf16[3,2304,256]{2,1,0:T(8,128)(2,1)} %bitcast.3, ...), custom_call_target="tpu_custom_call" | custom-call | tf_op jit(solution)/shard_map/pallas_call | solution.py:511
  74.7 4.3 %shard_map.74 = bf16[16,84,4,256]{3,2,1,0:T(4,128)(2,1)} custom-call(f32[2,5376,128]{2,1,0:T(8,128)} %get-tuple-element.7.z_hbm, f32[16,2,256]{2,1,0:T(2,128)} %get-tuple-element.8.stat_hbm, f32[3,2,256]{2,1,0:T(2,128)} %norm_hbm.1), custom_call_target="tpu_custom_call" | custom-call | tf_op jit(solution)/shard_map/pallas_call | solution.py:541

commit v5 on v4

--- a/solution.py
+++ b/solution.py
@@ -36,6 +36,10 @@
         flat = lax.rem(me + offset, n_group)
         return (my_pod, flat // n_sp, lax.rem(flat, n_sp))
 
+    barrier = pltpu.get_barrier_semaphore()
+    for i in range(1, n_group):
+        pl.semaphore_signal(barrier, inc=1, device_id=peer(i), device_id_type=MESH)
+
     row_copies = [pltpu.make_async_copy(img.at[:, r], nat.at[r + 1], in_sem.at[r]) for r in range(n_row)]
     for c in row_copies:
         c.start()
@@ -55,10 +59,6 @@
     for c in w_copies:
         c.start()
 
-    barrier = pltpu.get_barrier_semaphore()
-    for i in range(1, n_group):
-        pl.semaphore_signal(barrier, inc=1, device_id=peer(i), device_id_type=MESH)
-
     for p in range(3):
         wa_v[pl.ds(p * 4 * ch_a + 3 * ch_a, ch_a), 0:ch_a] = jnp.zeros((ch_a, ch_a), BF16)
         wa_v[pl.ds(p * 4 * ch_a, ch_a), ch_a:2 * ch_a] = jnp.zeros((ch_a, ch_a), BF16)
@@ -79,30 +79,37 @@
         nat[n_row + 1] = jnp.zeros((n_img, width, ch_a), BF16)
         nat[n_row + 2] = jnp.zeros((n_img, width, ch_a), BF16)
         act_b[n_out_row + 1] = jnp.zeros((w_out + 2, n_img, ch_b), BF16)
-
-    def image_halo(src_row, dst_row, dev, k):
+        act_a[n_row] = jnp.zeros((w_out + 1, n_img, 2 * ch_a), BF16)
+
+    x_split = width * 4 // 7 // 16 * 16
+    cols_x = width * 10 // 21 // 16 * 16
+    n_pair = cols_x // 2 - 1
+    n_far = n_pair + w_out * 22 // 84
+
+    def remote(src, dst, k, dev):
         return pltpu.make_async_remote_copy(
-            src_ref=img.at[:, src_row], dst_ref=nat.at[dst_row], send_sem=halo_in_send.at[k],
-            recv_sem=halo_in_recv.at[k], device_id=dev, device_id_type=MESH)
-
-    to_lower = image_halo(n_row - 1, 0, lower, 0)
-    to_upper0 = image_halo(0, n_row + 1, upper, 1)
-    cols_x = width * 4 // 7 // 16 * 16
-    n_pair = cols_x // 2 - 1
-    to_upper1 = pltpu.make_async_remote_copy(
-        src_ref=img.at[:, 1, pl.ds(0, cols_x)], dst_ref=nat.at[n_row + 2, :, pl.ds(0, cols_x)], send_sem=halo_in_send.at[2],
-        recv_sem=halo_in_recv.at[2], device_id=upper, device_id_type=MESH)
-    far = pl.ds(n_pair * n_img, (w_out - n_pair) * n_img)
-    to_upper_z = pltpu.make_async_remote_copy(
-        src_ref=zbuf.at[0, far], dst_ref=zbuf.at[n_row, far], send_sem=halo_in_send.at[3],
-        recv_sem=halo_in_recv.at[3], device_id=upper, device_id_type=MESH)
-
-    def transpose_row(k, cols=width):
+            src_ref=src, dst_ref=dst, send_sem=halo_in_send.at[k], recv_sem=halo_in_recv.at[k],
+            device_id=dev, device_id_type=MESH)
+
+    def image_halo(src_row, dst_row, dev, k, first, count):
+        cols = pl.ds(first, count)
+        return remote(nat.at[src_row + 1, :, cols], nat.at[dst_row, :, cols], k, dev)
+
+    x_parts = ((0, x_split), (x_split, width - x_split))
+    to_lower = [image_halo(n_row - 1, 0, lower, k, *x_parts[k]) for k in range(2)]
+    to_upper = [image_halo(0, n_row + 1, upper, 2 + k, *x_parts[k]) for k in range(2)]
+    to_upper.append(image_halo(1, n_row + 2, upper, 4, 0, cols_x))
+    mid = pl.ds(n_pair * n_img, (n_far - n_pair) * n_img)
+    to_upper_z = remote(zbuf.at[0, mid], zbuf.at[n_row, mid], 5, upper)
+    far = pl.ds(n_far, w_out - n_far)
+    to_upper_y = remote(act_a.at[0, far], act_a.at[n_row, far], 6, upper)
+
+    def transpose_row(k, first=0, cols=width):
         pitch = stage.shape[0] // n_img
 
         for i in range(n_img):
-            stage[pl.ds(i * pitch, cols), :] = nat[k, i, 0:cols].astype(F32)
-        for x in range(cols):
+            stage[pl.ds(i * pitch + first, cols), :] = nat[k, i, first:first + cols].astype(F32)
+        for x in range(first, first + cols):
             half = (x + 1) % 2
             img_t[k, (x + 1) // 2, :, half * ch_a:(half + 1) * ch_a] = (
                 stage[pl.ds(x, n_img, stride=pitch), :].astype(BF16))
@@ -111,11 +118,11 @@
         z3 = z_val.reshape(z_val.shape[0] // 8, 8, ch_b)
         return total[0] + jnp.sum(z3, axis=0), total[1] + jnp.sum(z3 * z3, axis=0)
 
-    def conv_a(r, rows=(0, 1, 2), pairs=w_out):
+    def conv_a(r, rows=(0, 1, 2), first=0, pairs=w_out):
         parts = []
         for p in rows:
             for k in range(2):
-                parts.append(img_t[r + p, pl.ds(k, pairs)].reshape(pairs * n_img, 2 * ch_a))
+                parts.append(img_t[r + p, pl.ds(k + first, pairs)].reshape(pairs * n_img, 2 * ch_a))
         w_val = wa_v[pl.ds(rows[0] * 4 * ch_a, len(rows) * 4 * ch_a)]
         return jnp.dot(jnp.concatenate(parts, axis=1), w_val, preferred_element_type=F32)
 
@@ -194,52 +201,59 @@
 
     with jax.named_scope("transpose"):
         lax.fori_loop(0, n_row, t_body, 0)
+    for c in w_copies[:18]:
+        c.wait()
+
+    def a_rows(first, count, total):
+        z_rows = [conv_a(first + j) for j in range(count)]
+        for j in range(count):
+            keep_z(first + j, z_rows[j])
+            total = fold(total, z_rows[j])
+        return total
+
     with jax.named_scope("barrier"):
         pl.semaphore_wait(barrier, n_group - 1)
 
     @pl.when(not_bottom)
     def _():
-        to_lower.start()
+        for c in to_lower:
+            c.start()
 
     @pl.when(not_top)
     def _():
-        to_upper0.start()
-        to_upper1.start()
-
-    for c in w_copies:
-        c.wait()
-
-    def a_body(i, total):
-        r = 1 + 2 * i
-        z_pair = [conv_a(r), conv_a(r + 1)]
-        for j in range(2):
-            keep_z(r + j, z_pair[j])
-            total = fold(total, z_pair[j])
-        return total
-
+        for c in to_upper:
+            c.start()
+
+    with jax.named_scope("conv_a_first"):
+        total = a_rows(1, 1, zeros)
     with jax.named_scope("conv_a"):
-        total = lax.fori_loop(0, (n_row - 4) // 2, a_body, zeros)
+        total = lax.fori_loop(0, (n_row - 4) // 2, lambda i, t: a_rows(2 + 2 * i, 2, t), total)
     with jax.named_scope("conv_a_part"):
-        total = a_body((n_row - 4) // 2, total)
+        total = a_rows(n_row - 2, 1, total)
         keep_z(0, conv_a(0, (1, 2)))
         keep_z(n_row - 1, conv_a(n_row - 1, (0, 1)))
-    with jax.named_scope("img_halo_wait"):
-        @pl.when(not_top)
-        def _():
-            to_lower.wait_recv()
-
-        @pl.when(not_bottom)
-        def _():
-            to_upper0.wait_recv()
-
-    with jax.named_scope("transpose_halo"):
-        transpose_row(0)
-        transpose_row(n_row + 1)
-    with jax.named_scope("conv_a_edge"):
-        for r, p in ((0, 0), (n_row - 1, 2)):
-            z_val = conv_a(r, (p,)) + zbuf[r]
-            keep_z(r, z_val)
-            total = fold(total, z_val)
+
+    pair_parts = ((0, (x_split - 1) // 2), ((x_split - 1) // 2, w_out - (x_split - 1) // 2))
+    for k in range(2):
+        with jax.named_scope("img_halo_wait"):
+            @pl.when(not_top)
+            def _():
+                to_lower[k].wait_recv()
+
+            @pl.when(not_bottom)
+            def _():
+                to_upper[k].wait_recv()
+
+        with jax.named_scope("transpose_halo"):
+            transpose_row(0, *x_parts[k])
+            transpose_row(n_row + 1, *x_parts[k])
+        with jax.named_scope("conv_a_edge"):
+            first, count = pair_parts[k]
+            rows = slice(first * n_img, (first + count) * n_img)
+            for r, p in ((0, 0), (n_row - 1, 2)):
+                z_val = conv_a(r, (p,), first, count) + zbuf[r, rows]
+                zbuf[r, rows] = z_val
+                total = fold(total, z_val)
     with jax.named_scope("send_stats"):
         copies = send_stats(0, total)
 
@@ -247,13 +261,15 @@
         def _():
             to_upper_z.start()
 
+    for c in w_copies[18:]:
+        c.wait()
     with jax.named_scope("img_halo_wait2"):
         @pl.when(not_bottom)
         def _():
-            to_upper1.wait_recv()
+            to_upper[2].wait_recv()
 
     with jax.named_scope("conv_a_extra"):
-        transpose_row(n_row + 2, cols_x)
+        transpose_row(n_row + 2, 0, cols_x)
         zbuf[n_row, 0:n_pair * n_img] = conv_a(n_row, pairs=n_pair)
     n_a = float(n_group * n_img * n_row * width)
     wide = lambda v: jnp.concatenate([v, v], axis=1)
@@ -264,8 +280,6 @@
 
     def norm_a_cols(r, k):
         y_val = normalize(zbuf[r, k * piece * n_img:(k + 1) * piece * n_img], coef_a)
-        if r == n_row:
-            y_val = jnp.where(is_bottom, jnp.zeros_like(y_val), y_val)
         act_a[r, pl.ds(k * piece, piece)] = y_val.reshape(piece, n_img, 2 * ch_a)
 
     def norm_a_row(r):
@@ -279,7 +293,13 @@
 
     with jax.named_scope("conv_down"):
         total = zeros
-        for r in range(3):
+        norm_a_row(0)
+
+        @pl.when(not_top)
+        def _():
+            to_upper_y.start()
+
+        for r in range(1, 3):
             norm_a_row(r)
         for r in range(n_out_row - 1):
             for k in range(n_piece):
@@ -291,17 +311,21 @@
         @pl.when(not_top)
         def _():
             to_upper_z.wait_send()
+            to_upper_y.wait_send()
 
         @pl.when(not_bottom)
         def _():
             to_upper_z.wait_recv()
+            to_upper_y.wait_recv()
 
     with jax.named_scope("conv_down_last"):
-        norm_a_row(n_row)
+        y_val = normalize(zbuf[n_row, 0:n_far * n_img], coef_a)
+        y_val = jnp.where(is_bottom, jnp.zeros_like(y_val), y_val)
+        act_a[n_row, pl.ds(0, n_far)] = y_val.reshape(n_far, n_img, 2 * ch_a)
         for k in range(n_piece):
             total = down_cols(n_out_row - 1, k, total)
 
-    late_cols = (n_early, (n_early + w_out) // 2, w_out)
+    late_cols = (n_early, (n_early + 2 * w_out) // 3, w_out)
     last_row = n_out_row - 1
 
     def early_copies(layer):
@@ -442,12 +466,13 @@
 
     @pl.when(not_bottom)
     def _():
-        to_lower.wait_send()
+        for c in to_lower:
+            c.wait_send()
 
     @pl.when(not_top)
     def _():
-        to_upper0.wait_send()
-        to_upper1.wait_send()
+        for c in to_upper:
+            c.wait_send()
 
 
 def finish_kernel(count, z_hbm, stat_hbm, norm_hbm, out, z_v, stat, norms, out_v, z_sem, small_sem, out_sem):
@@ -507,7 +532,7 @@
         vmem_spec = pl.BlockSpec(memory_space=pltpu.VMEM)
         dma = pltpu.SemaphoreType.DMA
         n_stats = 2 + n_layers_b
-        n_early = w_out // 3
+        n_early = w_out // 4
         z_val, stats = pl.pallas_call(
             functools.partial(stack_kernel, n_dp, n_sp, n_early),
             out_shape=(
@@ -530,7 +555,7 @@
                 pltpu.VMEM((n_layers_b, 9 * ch_b, ch_b), BF16),
                 pltpu.VMEM((n_stats, 2, ch_b), F32),
                 pltpu.VMEM((n_stats - 1, n_group, 2, ch_b), F32),
-                dma((n_row,)), dma((28,)), dma((4,)), dma((4,)),
+                dma((n_row,)), dma((28,)), dma((7,)), dma((7,)),
                 dma((n_stats, n_group)), dma((n_stats, n_group)),
                 dma((n_layers_b, 2, 2)), dma((n_layers_b, 2, 2)), dma((n_layers_b, 2)), dma((n_layers_b, 2)), dma, dma,
             ],

time: 79.3 us -> 76 us (0.958)
  Pallas kernels: 78.9 us -> 75.6 us
    pallas_call x1, Pallas kernels: 74.6 us -> 71.3 us  [local_stack(): pl.pallas_call(functools.partial(stack_kernel, n_dp, n_sp, n_early), out_...]
where the time goes in v5:
time: 76 us; the launch traced here: 75.8 us
  Pallas kernels  75.6 us (99%)
    pallas_call x1, Pallas kernels, local_stack(): pl.pallas_call(functools.partial(stack_kernel, n_dp, n_sp, n_early), out_...  71.3 us
    pallas_call x1, Pallas kernels, local_stack(): pl.pallas_call(functools.partial(finish_kernel, float(n_group * n_img * n...  4.26 us

profile of v5, /device:TPU:0, one launch (start us, length us, event | category | flops | bytes accessed | tf_op | source)
XLA Modules:
  0.0 75.8 jit_solution(13867238306262445622)
XLA Ops:
  0.0 71.3 %shard_map.73 = (f32[2,5376,128]{2,1,0:T(8,128)}, f32[16,2,256]{2,1,0:T(2,128)}) custom-call(bf16[16,8,168,128]{3,2,1,0:T(8,128)(2,1)} %img.1, bf16[3,3,128,128]{3,2,1,0:T(8,128)(2,1)} %bitcast.4, f32[1,2,128]{2,1,0:T(2,128)} %na.1, bf16[3,3,128,256]{3,2,1,0:T(8,128)(2,1)} %wd.1, f32[2,256]{1,0:T(2,128)} %nd.1, bf16[3,2304,256]{2,1,0:T(8,128)(2,1)} %bitcast.3, ...), custom_call_target="tpu_custom_call" | custom-call | tf_op jit(solution)/shard_map/pallas_call | solution.py:536
  71.3 4.3 %shard_map.74 = bf16[16,84,4,256]{3,2,1,0:T(4,128)(2,1)} custom-call(f32[2,5376,128]{2,1,0:T(8,128)} %get-tuple-element.7.z_hbm, f32[16,2,256]{2,1,0:T(2,128)} %get-tuple-element.8.stat_hbm, f32[3,2,256]{2,1,0:T(2,128)} %norm_hbm.1), custom_call_target="tpu_custom_call" | custom-call | tf_op jit(solution)/shard_map/pallas_call | solution.py:566

commit v6 on v5

--- a/solution.py
+++ b/solution.py
@@ -50,12 +50,12 @@
                 k = q + half
                 w_copies.append(pltpu.make_async_copy(
                     wa.at[p, q], wa_v.at[pl.ds(p * 4 * ch_a + k * ch_a, ch_a), pl.ds(half * ch_a, ch_a)],
-                    w_sem.at[len(w_copies)]))
+                    w_sem.at[0]))
     for p in range(3):
         for q in range(3):
             off = p * 2 * ch_a + q * ch_a if q < 2 else 6 * ch_a + p * ch_a
-            w_copies.append(pltpu.make_async_copy(wd.at[p, q], wd_v.at[pl.ds(off, ch_a)], w_sem.at[len(w_copies)]))
-    w_copies.append(pltpu.make_async_copy(wb, wb_v, w_sem.at[len(w_copies)]))
+            w_copies.append(pltpu.make_async_copy(wd.at[p, q], wd_v.at[pl.ds(off, ch_a)], w_sem.at[1]))
+    w_copies.append(pltpu.make_async_copy(wb, wb_v, w_sem.at[2]))
     for c in w_copies:
         c.start()
 
@@ -166,14 +166,16 @@
         copies = []
         for i in range(1, n_group):
             copies.append(pltpu.make_async_remote_copy(
-                src_ref=stat_src.at[layer], dst_ref=slot, send_sem=stat_send.at[layer, i],
-                recv_sem=stat_recv.at[layer, i], device_id=peer(i), device_id_type=MESH))
+                src_ref=stat_src.at[layer], dst_ref=slot, send_sem=stat_send.at[layer],
+                recv_sem=stat_recv.at[layer], device_id=peer(i), device_id_type=MESH))
         for c in copies:
             c.start()
+        all_slots = (stat_out if last else stat_dst.at[layer]).at[pl.ds(0, n_group - 1)]
+        waits = [pltpu.make_async_copy(all_slots, all_slots, sem.at[layer]) for sem in (stat_send, stat_recv)]
         if last:
-            copies.append(pltpu.make_async_copy(stat_src.at[layer], slot, own_sem))
-            copies[-1].start()
-        return copies
+            waits.append(pltpu.make_async_copy(stat_src.at[layer], slot, own_sem))
+            waits[-1].start()
+        return waits
 
     def finish_stats(layer, copies, gamma, beta, count):
         with jax.named_scope("stats_wait"):
@@ -201,8 +203,8 @@
 
     with jax.named_scope("transpose"):
         lax.fori_loop(0, n_row, t_body, 0)
-    for c in w_copies[:18]:
-        c.wait()
+    wa_part = wa_v.at[pl.ds(0, 9 * ch_a)]
+    pltpu.make_async_copy(wa_part, wa_part, w_sem.at[0]).wait()
 
     def a_rows(first, count, total):
         z_rows = [conv_a(first + j) for j in range(count)]
@@ -261,8 +263,8 @@
         def _():
             to_upper_z.start()
 
-    for c in w_copies[18:]:
-        c.wait()
+    pltpu.make_async_copy(wd_v, wd_v, w_sem.at[1]).wait()
+    w_copies[-1].wait()
     with jax.named_scope("img_halo_wait2"):
         @pl.when(not_bottom)
         def _():
@@ -342,10 +344,10 @@
         cols = pl.ds(1 + late_cols[k], late_cols[k + 1] - late_cols[k])
         up = pltpu.make_async_remote_copy(
             src_ref=act_b.at[1, cols], dst_ref=act_b.at[n_out_row + 1, cols],
-            send_sem=halo_send.at[layer, k, 1], recv_sem=halo_recv.at[layer, k, 1], device_id=upper, device_id_type=MESH)
+            send_sem=halo_send.at[k, 1], recv_sem=halo_recv.at[k, 1], device_id=upper, device_id_type=MESH)
         down = pltpu.make_async_remote_copy(
             src_ref=act_b.at[n_out_row, cols], dst_ref=act_b.at[0, cols],
-            send_sem=halo_send.at[layer, k, 0], recv_sem=halo_recv.at[layer, k, 0], device_id=lower, device_id_type=MESH)
+            send_sem=halo_send.at[k, 0], recv_sem=halo_recv.at[k, 0], device_id=lower, device_id_type=MESH)
         return up, down
 
     def start_both(up, down):
@@ -493,7 +495,7 @@
     for c in small:
         c.start()
     for k in range(n_chunk):
-        z_copy(k).start()
+        z_copy(k).start(priority=1)
     for c in small:
         c.wait()
     norm = norms[norms.shape[0] - 1]
@@ -555,9 +557,9 @@
                 pltpu.VMEM((n_layers_b, 9 * ch_b, ch_b), BF16),
                 pltpu.VMEM((n_stats, 2, ch_b), F32),
                 pltpu.VMEM((n_stats - 1, n_group, 2, ch_b), F32),
-                dma((n_row,)), dma((28,)), dma((7,)), dma((7,)),
-                dma((n_stats, n_group)), dma((n_stats, n_group)),
-                dma((n_layers_b, 2, 2)), dma((n_layers_b, 2, 2)), dma((n_layers_b, 2)), dma((n_layers_b, 2)), dma, dma,
+                dma((n_row,)), dma((3,)), dma((7,)), dma((7,)),
+                dma((n_stats,)), dma((n_stats,)),
+                dma((2, 2)), dma((2, 2)), dma((n_layers_b, 2)), dma((n_layers_b, 2)), dma, dma,
             ],
             compiler_params=pltpu.CompilerParams(
                 collective_id=0, has_side_effects=True, vmem_limit_bytes=67043328),

time: 76 us -> 73.8 us (0.971)
  Pallas kernels: 75.6 us -> 73.4 us
    pallas_call x1, Pallas kernels: 71.3 us -> 69.5 us  [local_stack(): pl.pallas_call(functools.partial(stack_kernel, n_dp, n_sp, n_early), out_...]
where the time goes in v6:
time: 73.8 us; the launch traced here: 73.6 us
  Pallas kernels  73.4 us (99%)
    pallas_call x1, Pallas kernels, local_stack(): pl.pallas_call(functools.partial(stack_kernel, n_dp, n_sp, n_early), out_...  69.5 us
    pallas_call x1, Pallas kernels, local_stack(): pl.pallas_call(functools.partial(finish_kernel, float(n_group * n_img * n...  3.88 us

profile of v6, /device:TPU:0, one launch (start us, length us, event | category | flops | bytes accessed | tf_op | source)
XLA Modules:
  0.0 73.6 jit_solution(12136948336907225082)
XLA Ops:
  0.0 69.5 %shard_map.73 = (f32[2,5376,128]{2,1,0:T(8,128)}, f32[16,2,256]{2,1,0:T(2,128)}) custom-call(bf16[16,8,168,128]{3,2,1,0:T(8,128)(2,1)} %img.1, bf16[3,3,128,128]{3,2,1,0:T(8,128)(2,1)} %bitcast.4, f32[1,2,128]{2,1,0:T(2,128)} %na.1, bf16[3,3,128,256]{3,2,1,0:T(8,128)(2,1)} %wd.1, f32[2,256]{1,0:T(2,128)} %nd.1, bf16[3,2304,256]{2,1,0:T(8,128)(2,1)} %bitcast.3, ...), custom_call_target="tpu_custom_call" | custom-call | tf_op jit(solution)/shard_map/pallas_call | solution.py:538
  69.5 3.9 %shard_map.74 = bf16[16,84,4,256]{3,2,1,0:T(4,128)(2,1)} custom-call(f32[2,5376,128]{2,1,0:T(8,128)} %get-tuple-element.7.z_hbm, f32[16,2,256]{2,1,0:T(2,128)} %get-tuple-element.8.stat_hbm, f32[3,2,256]{2,1,0:T(2,128)} %norm_hbm.1), custom_call_target="tpu_custom_call" | custom-call | tf_op jit(solution)/shard_map/pallas_call | solution.py:568

commit v7 on v6

--- a/solution.py
+++ b/solution.py
@@ -327,7 +327,7 @@
         for k in range(n_piece):
             total = down_cols(n_out_row - 1, k, total)
 
-    late_cols = (n_early, (n_early + 2 * w_out) // 3, w_out)
+    late_cols = (n_early, (n_early + 3 * w_out) // 4, w_out)
     last_row = n_out_row - 1
 
     def early_copies(layer):
@@ -515,7 +515,7 @@
                 out_v[:, x, :, lanes] = y_val.reshape(n_img, n_out_row, 128)
             return carry
 
-        lax.fori_loop(k * chunk, (k + 1) * chunk, out_body, 0, unroll=3)
+        lax.fori_loop(k * chunk, (k + 1) * chunk, out_body, 0, unroll=7)
         out_copy(k).start()
     for k in range(n_chunk):
         out_copy(k).wait()
@@ -534,7 +534,7 @@
         vmem_spec = pl.BlockSpec(memory_space=pltpu.VMEM)
         dma = pltpu.SemaphoreType.DMA
         n_stats = 2 + n_layers_b
-        n_early = w_out // 4
+        n_early = w_out * 22 // 84
         z_val, stats = pl.pallas_call(
             functools.partial(stack_kernel, n_dp, n_sp, n_early),
             out_shape=(

time: 73.8 us -> 73.6 us (level)
  no operation moved by 1% of the time
where the time goes in v7:
time: 73.6 us; the launch traced here: 73.4 us
  Pallas kernels  73.2 us (99%)
    pallas_call x1, Pallas kernels, local_stack(): pl.pallas_call(functools.partial(stack_kernel, n_dp, n_sp, n_early), out_...  69.3 us
    pallas_call x1, Pallas kernels, local_stack(): pl.pallas_call(functools.partial(finish_kernel, float(n_group * n_img * n...  3.85 us

profile of v7, /device:TPU:0, one launch (start us, length us, event | category | flops | bytes accessed | tf_op | source)
XLA Modules:
  0.0 73.4 jit_solution(108734993353259101)
XLA Ops:
  0.0 69.3 %shard_map.73 = (f32[2,5376,128]{2,1,0:T(8,128)}, f32[16,2,256]{2,1,0:T(2,128)}) custom-call(bf16[16,8,168,128]{3,2,1,0:T(8,128)(2,1)} %img.1, bf16[3,3,128,128]{3,2,1,0:T(8,128)(2,1)} %bitcast.4, f32[1,2,128]{2,1,0:T(2,128)} %na.1, bf16[3,3,128,256]{3,2,1,0:T(8,128)(2,1)} %wd.1, f32[2,256]{1,0:T(2,128)} %nd.1, bf16[3,2304,256]{2,1,0:T(8,128)(2,1)} %bitcast.3, ...), custom_call_target="tpu_custom_call" | custom-call | tf_op jit(solution)/shard_map/pallas_call | solution.py:538
  69.3 3.8 %shard_map.74 = bf16[16,84,4,256]{3,2,1,0:T(4,128)(2,1)} custom-call(f32[2,5376,128]{2,1,0:T(8,128)} %get-tuple-element.7.z_hbm, f32[16,2,256]{2,1,0:T(2,128)} %get-tuple-element.8.stat_hbm, f32[3,2,256]{2,1,0:T(2,128)} %norm_hbm.1), custom_call_target="tpu_custom_call" | custom-call | tf_op jit(solution)/shard_map/pallas_call | solution.py:568
